TPU v7x, 16 devices: a whole 2x2x2 slice. The times are simulated.
16 devices in a mesh: dp: 4 (over z, y), ep: 4 (over x, core).
Axes of the slice: x: 2, y: 2, z: 2, core: 2. Of those that a mesh axis runs over, the one named last changes fastest.
Arguments:
- grad_y: bfloat16 [1024, 1024], P(('dp', 'ep')), parts along dimension 0
- gate_vals: float32 [1024, 8], P(('dp', 'ep')), parts along dimension 0
- topk_idx: int32 [1024, 8], P(('dp', 'ep')), parts along dimension 0
- slot_ids: int32 [1024, 8], P(('dp', 'ep')), parts along dimension 0
- pair_counts: int32 [16, 32], P(('dp', 'ep')), parts along dimension 0
- y_routed: bfloat16 [1024, 8, 1024], P(('dp', 'ep')), parts along dimension 0
- x_disp: bfloat16 [128, 128, 1024], P(('dp', 'ep')), parts along dimension 0
- h_gate: bfloat16 [128, 128, 512], P(('dp', 'ep')), parts along dimension 0
- h_up: bfloat16 [128, 128, 512], P(('dp', 'ep')), parts along dimension 0
- w_gate: bfloat16 [32, 1024, 512], P('ep')
- w_up: bfloat16 [32, 1024, 512], P('ep')
- w_down: bfloat16 [32, 512, 1024], P('ep')
Outputs:
- output 1: bfloat16 [1024, 1024], P(('dp', 'ep')), parts along dimension 0
- output 2: float32 [1024, 8], P(('dp', 'ep')), parts along dimension 0
- output 3: float32 [128, 1024, 512], P(('dp', 'ep')), parts along dimension 0
- output 4: float32 [128, 1024, 512], P(('dp', 'ep')), parts along dimension 0
- output 5: float32 [128, 512, 1024], P(('dp', 'ep')), parts along dimension 0
There are 4 independent parts. A program takes and returns all parts, laid end to end along the dimension named above; an argument that names none is the same for every part.
All inputs are finite; a program needn't handle non-finite values.
Results may differ from a plain program's by a relative error of at most 0.0149207.
Values are sent between devices in bfloat16 or wider.
A program may use at most 1 GiB of HBM per device.

v0:
```python
import jax
import jax.numpy as jnp
from jax import lax
from jax.sharding import PartitionSpec as P


def build_send(grad_y, gate_vals, topk_idx, slot_ids, n_exp, cap_rows):
    tok_dev, top_k = topk_idx.shape
    dest_row = jnp.where(slot_ids >= 0, topk_idx * cap_rows + slot_ids, n_exp * cap_rows).reshape(-1)
    row_source = jnp.full((n_exp * cap_rows,), tok_dev * top_k, jnp.int32).at[dest_row].set(jnp.arange(tok_dev * top_k, dtype=jnp.int32), mode="drop")
    dy_rows = jnp.take(grad_y, row_source // top_k, axis=0, mode="fill", fill_value=0)
    gate_rows = jnp.take(gate_vals.reshape(-1), row_source, mode="fill", fill_value=0)
    return (gate_rows[:, None] * dy_rows).astype(jnp.bfloat16).reshape(n_exp, cap_rows, grad_y.shape[1])


def gather_back(ret_rows, topk_idx, slot_ids, cap_rows):
    tok_dev, top_k = topk_idx.shape
    src_row = jnp.where(slot_ids >= 0, topk_idx * cap_rows + slot_ids, ret_rows.shape[0]).reshape(-1)
    picked = jnp.take(ret_rows, src_row, axis=0, mode="fill", fill_value=0).reshape(tok_dev, top_k, ret_rows.shape[1])
    return jnp.sum(picked, axis=1, dtype=jnp.float32).astype(jnp.bfloat16)


def expert_grads(grad_rows, x_rows, hg_rows, hu_rows, w_gate, w_up, w_down):
    grad_hidden = jnp.einsum("erd,efd->erf", grad_rows, w_down, preferred_element_type=jnp.float32).astype(jnp.bfloat16)
    gate_f = hg_rows.astype(jnp.float32)
    up_f = hu_rows.astype(jnp.float32)
    gate_sig = jax.nn.sigmoid(gate_f)
    gate_act = gate_f * gate_sig
    hidden_act = (gate_act * up_f).astype(jnp.bfloat16)
    grad_h = grad_hidden.astype(jnp.float32)
    grad_hgate = (grad_h * up_f * gate_sig * (1.0 + gate_f * (1.0 - gate_sig))).astype(jnp.bfloat16)
    grad_hup = (grad_h * gate_act).astype(jnp.bfloat16)
    grad_wdown = jnp.einsum("erf,erd->efd", hidden_act, grad_rows, preferred_element_type=jnp.float32)
    grad_wgate = jnp.einsum("erd,erf->edf", x_rows, grad_hgate, preferred_element_type=jnp.float32)
    grad_wup = jnp.einsum("erd,erf->edf", x_rows, grad_hup, preferred_element_type=jnp.float32)
    grad_disp = (jnp.einsum("erf,edf->erd", grad_hgate, w_gate, preferred_element_type=jnp.float32) + jnp.einsum("erf,edf->erd", grad_hup, w_up, preferred_element_type=jnp.float32)).astype(jnp.bfloat16)
    return grad_disp, grad_wgate, grad_wup, grad_wdown


def solution(mesh):
    n_dev = mesh.shape["ep"]
    rows_spec = P(("dp", "ep"), None)
    cube_spec = P(("dp", "ep"), None, None)
    weight_spec = P("ep", None, None)

    def local_step(grad_y, gate_vals, topk_idx, slot_ids, pair_counts, y_routed, x_disp, h_gate, h_up, w_gate, w_up, w_down):
        n_loc = w_gate.shape[0]
        n_exp = n_loc * n_dev
        cap_rows = x_disp.shape[1] // n_dev
        model_dim = grad_y.shape[1]
        grad_gate = jnp.einsum("td,tkd->tk", grad_y, y_routed, preferred_element_type=jnp.float32)
        send_rows = build_send(grad_y, gate_vals, topk_idx, slot_ids, n_exp, cap_rows)
        recv_rows = lax.all_to_all(send_rows.reshape(n_dev, n_loc, cap_rows, model_dim), "ep", 0, 1)
        recv_counts = lax.all_to_all(pair_counts.reshape(n_dev, n_loc), "ep", 0, 1)
        keep_row = lax.broadcasted_iota(jnp.int32, (n_loc, n_dev, cap_rows), 2) < recv_counts[:, :, None]
        grad_rows = jnp.where(keep_row[..., None], recv_rows, jnp.zeros((), jnp.bfloat16)).reshape(n_loc, n_dev * cap_rows, model_dim)
        grad_disp, grad_wgate, grad_wup, grad_wdown = expert_grads(grad_rows, x_disp, h_gate, h_up, w_gate, w_up, w_down)
        ret_rows = lax.all_to_all(grad_disp.reshape(n_loc, n_dev, cap_rows, model_dim), "ep", 1, 0)
        grad_x = gather_back(ret_rows.reshape(n_exp * cap_rows, model_dim), topk_idx, slot_ids, cap_rows)
        return grad_x, grad_gate, grad_wgate, grad_wup, grad_wdown

    return jax.shard_map(local_step, mesh=mesh, in_specs=(rows_spec, rows_spec, rows_spec, rows_spec, rows_spec, cube_spec, cube_spec, cube_spec, cube_spec, weight_spec, weight_spec, weight_spec), out_specs=(rows_spec, rows_spec, cube_spec, cube_spec, cube_spec), check_vma=False)
```

profile of v0, /device:TPU:0, one launch (start us, length us, event | category | flops | bytes accessed | tf_op | source)
XLA Modules:
  0.0 156.4 jit_solution(9923027693180456114)
XLA Ops:
  1.2 1.4 reduce.4
  3.3 4.5 %all-to-all-start = ((s32[4,8,1]{1,2,0:T(1,128)}), s32[4,8,1]{1,2,0:T(1,128)S(1)}, u32[]{:S(2)}, u32[]{:S(2)}) async-start(s32[4,8,1]{1,2,0:T(1,128)} %bitcast), calls=%async_computation | async-start | bytes 4096 | tf_op jit(solution)/shard_map/all_to_all | solution.py:54
  8.7 2.4 %scatter_custom_fusion = s32[1024]{0:T(1024)S(1)} fusion(s32[512]{0:T(512)S(1)} %bitcast.43, s32[512]{0:T(512)S(1)} %iota.18, s32[]{:T(128)} %constant.61.clone.1), kind=kCustom, calls=%fused_computation.51 | custom fusion | bytes 4100 | tf_op jit(solution)/shard_map/scatter | solution.py:10
  11.2 0.8 copy.53
  12.0 6.9 %gather_fusion = f32[1024]{0:T(1024)S(1)} fusion(f32[512]{0:T(512)S(1)} %reshape.116, s32[1024]{0:T(1024)S(1)} %get-tuple-element.27), kind=kCustom, calls=%fused_computation | custom fusion | bytes 12288 | tf_op jit(solution)/shard_map/jit(_take)/gather | solution.py:12
  19.1 5.3 %gather_fusion.1 = bf16[1024,1024]{1,0:T(8,128)(2,1)} fusion(bf16[64,1024]{1,0:T(8,128)(2,1)S(1)} %copy-done.1, s32[1024]{0:T(1024)S(1)} %get-tuple-element.28), kind=kCustom, calls=%fused_computation.1 | custom fusion | bytes 4198400 | tf_op jit(solution)/shard_map/jit(_take)/gather | solution.py:11
  24.4 3.5 %multiply_convert_fusion = bf16[4,8,1,32,1024]{4,3,1,2,0:T(8,128)(2,1)} fusion(bf16[4,8,1,32,1024]{4,3,1,2,0:T(8,128)(2,1)} %bitcast.38, f32[4,8,32]{2,1,0:T(8,128)S(1)} %mul.43, pred[4,8,32]{2,1,0:T(8,128)(4,1)S(1)} %broadcast_in_dim.61), kind=kLoop, calls=%fused_computation.7 | loop fusion | flops 4194304 | bytes 4199424 | tf_op jit(solution)/shard_map/convert_element_type | solution.py:13
  27.9 4.4 %all-to-all-start.1 = ((bf16[4,8,1,32,1024]{4,3,1,2,0:T(8,128)(2,1)}), bf16[4,8,1,32,1024]{4,3,1,2,0:T(8,128)(2,1)}, u32[]{:S(2)}, u32[]{:S(2)}) async-start(bf16[4,8,1,32,1024]{4,3,1,2,0:T(8,128)(2,1)} %multiply_convert_fusion), calls=%async_computation.1 | async-start | bytes 4194304 | tf_op jit(solution)/shard_map/all_to_all | solution.py:53
  32.5 2.0 %fusion.16 = f32[64,1,8]{2,1,0:T(1,128)S(1)} fusion(bf16[64,8,1024]{2,1,0:T(8,128)(2,1)} %param.17, bf16[64,1024,1]{1,0,2:T(8,128)(2,1)S(1)} %bitcast.37), kind=kOutput, calls=%fused_computation.31 | convolution fusion | flops 1048576 | bytes 1181696 | tf_op jit(solution)/shard_map/td,tkd->tk/dot_general | solution.py:51
  35.4 22.3 %all-to-all-done.1 = bf16[4,8,1,32,1024]{4,3,1,2,0:T(8,128)(2,1)} async-done(((bf16[4,8,1,32,1024]{4,3,1,2,0:T(8,128)(2,1)}), bf16[4,8,1,32,1024]{4,3,1,2,0:T(8,128)(2,1)}, u32[]{:S(2)}, u32[]{:S(2)}) %all-to-all-start.1) | async-done | bytes 2097184 | tf_op jit(solution)/shard_map/all_to_all | solution.py:53
  57.8 1.8 %copy.55 = bf16[4,8,1,32,1024]{4,3,0,1,2:T(8,128)(2,1)S(1)} copy(bf16[4,8,1,32,1024]{4,3,1,2,0:T(8,128)(2,1)} %all-to-all-done.1) | data formatting | bytes 4194304 | tf_op jit(solution)/shard_map/all_to_all | solution.py:53
  59.5 1.3 copy-done.3
  60.9 6.4 %fusion.11 = bf16[8,128,512]{2,1,0:T(8,128)(2,1)S(1)} fusion(bf16[8,512,1024]{2,1,0:T(8,128)(2,1)} %param.23, bf16[8,128,1024]{2,1,0:T(8,128)(2,1)S(1)} %bitcast.39, pred[8,128]{1,0:T(8,128)(4,1)S(1)} %broadcast_compare_fusion), kind=kOutput, calls=%fused_computation.26 | convolution fusion | flops 1075314688 | bytes 11535360 | tf_op jit(solution)/shard_map/erd,efd->erf/dot_general | solution.py:24
  67.4 8.7 %fusion.29 = f32[8,128,1024]{2,1,0:T(8,128)} fusion(bf16[8,1024,512]{2,1,0:T(8,128)(2,1)} %param.21, bf16[8,128,512]{2,1,0:T(8,128)(2,1)S(1)} %copy-done.5, bf16[8,128,512]{2,1,0:T(8,128)(2,1)S(1)} %fusion.11, bf16[8,128,512]{2,1,0:T(8,128)(2,1)S(1)} %copy-done.2), kind=kOutput, calls=%fused_computation.57 | convolution fusion | flops 1080557568 | bytes 15728640 | tf_op jit(solution)/shard_map/erf,edf->erd/dot_general | solution.py:36
  76.1 5.1 %add_convert_fusion = bf16[8,128,1024]{2,1,0:T(8,128)(2,1)S(1)} fusion(f32[8,128,1024]{2,1,0:T(8,128)} %fusion.29, bf16[8,1024,512]{2,1,0:T(8,128)(2,1)S(1)} %bitcast.47, bf16[8,128,512]{2,1,0:T(8,128)(2,1)S(1)} %fusion.11, bf16[8,128,512]{2,1,0:T(8,128)(2,1)S(1)} %copy-done.2), kind=kOutput, calls=%fused_computation.6 | convolution fusion | flops 1080033280 | bytes 16777216 | tf_op jit(solution)/shard_map/erf,edf->erd/dot_general | solution.py:36
  81.1 1.6 copy.56
  82.7 4.6 %all-to-all-start.2 = ((bf16[1,8,4,32,1024]{4,3,1,0,2:T(8,128)(2,1)}), bf16[1,8,4,32,1024]{4,3,1,0,2:T(8,128)(2,1)}, u32[]{:S(2)}, u32[]{:S(2)}) async-start(bf16[1,8,4,32,1024]{4,3,1,0,2:T(8,128)(2,1)} %copy.56), calls=%async_computation.2 | async-start | bytes 4194304 | tf_op jit(solution)/shard_map/all_to_all | solution.py:58
  87.3 10.1 %convolution_bitcast_fusion.1 = f32[8,1024,512]{1,2,0:T(8,128)} fusion(bf16[8,128,1024]{2,1,0:T(8,128)(2,1)S(1)} %copy-done, bf16[8,128,512]{2,1,0:T(8,128)(2,1)} %param.20, bf16[8,128,512]{2,1,0:T(8,128)(2,1)} %copy-done.4, bf16[8,128,512]{2,1,0:T(8,128)(2,1)S(1)} %copy-done.2), kind=kOutput, calls=%fused_computation.5 | convolution fusion | flops 1080557568 | bytes 22020096 | tf_op jit(solution)/shard_map/erd,erf->edf/dot_general | solution.py:34
  97.4 16.4 %copy.60 = f32[8,1024,512]{2,1,0:T(8,128)} copy(f32[8,1024,512]{1,2,0:T(8,128)} %convolution_bitcast_fusion.1) | data formatting | bytes 33554432
  113.9 9.8 %convolution_bitcast_fusion = f32[8,1024,512]{1,2,0:T(8,128)} fusion(bf16[8,128,1024]{2,1,0:T(8,128)(2,1)S(1)} %copy-done, bf16[8,128,512]{2,1,0:T(8,128)(2,1)} %copy-done.4, bf16[8,128,512]{2,1,0:T(8,128)(2,1)S(1)} %copy-done.2), kind=kOutput, calls=%fused_computation.4 | convolution fusion | flops 1077936128 | bytes 20971520 | tf_op jit(solution)/shard_map/erd,erf->edf/dot_general | solution.py:35
  123.6 16.4 %copy.61 = f32[8,1024,512]{2,1,0:T(8,128)} copy(f32[8,1024,512]{1,2,0:T(8,128)} %convolution_bitcast_fusion) | data formatting | bytes 33554432
  140.1 10.5 %fusion.9 = f32[8,512,1024]{2,1,0:T(8,128)} fusion(bf16[8,128,1024]{2,1,0:T(8,128)(2,1)} %bitcast.40, pred[8,128]{1,0:T(8,128)(4,1)S(1)} %broadcast_compare_fusion, bf16[8,128,512]{2,1,0:T(8,128)(2,1)} %param.20, bf16[8,128,512]{2,1,0:T(8,128)(2,1)S(1)} %copy-done.2), kind=kOutput, calls=%fused_computation.24 | convolution fusion | flops 1078984704 | bytes 20972544 | tf_op jit(solution)/shard_map/erf,erd->efd/dot_general | solution.py:33
  150.6 4.6 %gather_fusion.2 = bf16[512,1024]{1,0:T(8,128)(2,1)S(1)} fusion(bf16[1024,1024]{1,0:T(8,128)(2,1)} %bitcast.13, s32[1024]{0:T(1024)S(1)} %pad_clamp_fusion), kind=kCustom, calls=%fused_computation.2 | custom fusion | bytes 2099200 | tf_op jit(solution)/shard_map/jit(_take)/gather | solution.py:19
  155.2 1.2 fusion.13
  (40 shorter events, 3.5 us)
Async XLA Ops:
  0.6 86.7 %copy-start = (bf16[8,128,1024]{2,1,0:T(8,128)(2,1)S(1)}, bf16[8,128,1024]{2,1,0:T(8,128)(2,1)}, u32[]{:S(2)}) copy-start(bf16[8,128,1024]{2,1,0:T(8,128)(2,1)} %param.18) | copy-start | bytes 6291460
  3.3 24.6 %all-to-all-start = ((s32[4,8,1]{1,2,0:T(1,128)}), s32[4,8,1]{1,2,0:T(1,128)S(1)}, u32[]{:S(2)}, u32[]{:S(2)}) async-start(s32[4,8,1]{1,2,0:T(1,128)} %bitcast), calls=%async_computation | async-start | bytes 4096 | tf_op jit(solution)/shard_map/all_to_all | solution.py:54
  12.0 7.1 %copy-start.1 = (bf16[64,1024]{1,0:T(8,128)(2,1)S(1)}, bf16[64,1024]{1,0:T(8,128)(2,1)}, u32[]{:S(2)}) copy-start(bf16[64,1024]{1,0:T(8,128)(2,1)} %param.12) | copy-start | bytes 393220
  27.9 29.9 %all-to-all-start.1 = ((bf16[4,8,1,32,1024]{4,3,1,2,0:T(8,128)(2,1)}), bf16[4,8,1,32,1024]{4,3,1,2,0:T(8,128)(2,1)}, u32[]{:S(2)}, u32[]{:S(2)}) async-start(bf16[4,8,1,32,1024]{4,3,1,2,0:T(8,128)(2,1)} %multiply_convert_fusion), calls=%async_computation.1 | async-start | bytes 4194304 | tf_op jit(solution)/shard_map/all_to_all | solution.py:53
  59.5 1.3 copy-start.3
  60.9 6.5 %copy-start.2 = (bf16[8,128,512]{2,1,0:T(8,128)(2,1)S(1)}, bf16[8,128,512]{2,1,0:T(8,128)(2,1)}, u32[]{:S(2)}) copy-start(bf16[8,128,512]{2,1,0:T(8,128)(2,1)} %param.19) | copy-start | bytes 3145732
  60.9 6.5 %copy-start.5 = (bf16[8,128,512]{2,1,0:T(8,128)(2,1)S(1)}, bf16[8,128,512]{2,1,0:T(8,128)(2,1)}, u32[]{:S(2)}) copy-start(bf16[8,128,512]{2,1,0:T(8,128)(2,1)} %param.20) | copy-start | bytes 3145732
  60.9 15.2 %slice-start = ((s8[8388608]{0:T(1024)(128)(4,1)}), s8[4194304]{0:T(1024)(128)(4,1)S(1)}, s32[]{:S(2)}) async-start(s8[8388608]{0:T(1024)(128)(4,1)} %bitcast.46), calls=%async_computation.3 | async-start | bytes 8388608
  67.3 8.7 %copy-start.4 = (bf16[8,128,512]{2,1,0:T(8,128)(2,1)}, bf16[8,128,512]{2,1,0:T(8,128)(2,1)S(1)}, u32[]{:S(2)}) copy-start(bf16[8,128,512]{2,1,0:T(8,128)(2,1)S(1)} %fusion.11) | copy-start | bytes 3145732
  67.4 8.7 %slice-start.1 = ((s8[8388608]{0:T(1024)(128)(4,1)}), s8[4194304]{0:T(1024)(128)(4,1)S(1)}, s32[]{:S(2)}) async-start(s8[8388608]{0:T(1024)(128)(4,1)} %bitcast.46), calls=%async_computation.4 | async-start | bytes 8388608
  82.7 67.9 %all-to-all-start.2 = ((bf16[1,8,4,32,1024]{4,3,1,0,2:T(8,128)(2,1)}), bf16[1,8,4,32,1024]{4,3,1,0,2:T(8,128)(2,1)}, u32[]{:S(2)}, u32[]{:S(2)}) async-start(bf16[1,8,4,32,1024]{4,3,1,0,2:T(8,128)(2,1)} %copy.56), calls=%async_computation.2 | async-start | bytes 4194304 | tf_op jit(solution)/shard_map/all_to_all | solution.py:58
where the time goes:
time: 158 us; the launch traced here: 156 us
  local copies, waits for them, and re-layouts  60.2 us (38%)
  matrix products  52.5 us (33%)
  waiting for transfers between devices  22.3 us (14%)
  starting transfers between devices  13.6 us (9%)
  other arithmetic  6.9 us (4%)
    unnamed x20, local copies, waits for them, and re-layouts  35.5 us
    all_to_all x1, waiting for transfers between devices, local_step(): lax.all_to_all(send_rows.reshape(n_dev, n_loc, cap_rows, model_dim), 'ep'...  22.3 us
    dot_general x1, matrix products, expert_grads(): jnp.einsum('erf,erd->efd', hidden_act, grad_rows, preferred_element_type=...  10.5 us
    dot_general x1, matrix products, expert_grads(): jnp.einsum('erd,erf->edf', x_rows, grad_hgate, preferred_element_type=jnp...  10.1 us
    dot_general x1, matrix products, expert_grads(): jnp.einsum('erd,erf->edf', x_rows, grad_hup, preferred_element_type=jnp.f...  9.79 us
    dot_general x1, matrix products, expert_grads(): jnp.einsum('erf,edf->erd', grad_hgate, w_gate, preferred_element_type=jnp...  8.67 us
    gather x1, local copies, waits for them, and re-layouts, build_send(): jnp.take(gate_vals.reshape(-1), row_source, mode='fill', fill_value=0)  6.87 us
    dot_general x1, matrix products, expert_grads(): jnp.einsum('erd,efd->erf', grad_rows, w_down, preferred_element_type=jnp....  6.45 us
  transfers between devices with their start and end apart: 3, of which 1 were waited for; matrix products, arithmetic and copies ran while one was open for 55% of the time, Pallas kernels for 0%

commit v1 on v0

v1 whole, which is shorter than its diff:
```python
import functools

import jax
import jax.numpy as jnp
from jax import lax
from jax.experimental import pallas as pl
from jax.experimental.pallas import tpu as pltpu
from jax.sharding import PartitionSpec as P

MESH = pl.DeviceIdType.MESH
F32 = jnp.float32
BF16 = jnp.bfloat16


def gather_kernel(n_dev, *refs):
    n_arr = 5
    ins, outs = refs[:n_arr], refs[n_arr:2 * n_arr]
    local_sem, send_sem, recv_sem = refs[2 * n_arr:]
    me = lax.axis_index("ep")
    local = [pltpu.make_async_copy(ins[i], outs[i].at[0], local_sem.at[i]) for i in range(n_arr)]
    for cp in local:
        cp.start()
    barrier = pltpu.get_barrier_semaphore()
    for k in range(1, n_dev):
        pl.semaphore_signal(barrier, inc=1, device_id={"ep": me ^ k}, device_id_type=MESH)
    pl.semaphore_wait(barrier, n_dev - 1)
    for cp in local:
        cp.wait()

    def remote(i, k, src_slot, dst_slot):
        return pltpu.make_async_remote_copy(
            src_ref=outs[i].at[src_slot], dst_ref=outs[i].at[dst_slot],
            send_sem=send_sem.at[i, dst_slot], recv_sem=recv_sem.at[i, dst_slot],
            device_id={"ep": me ^ k}, device_id_type=MESH)

    far = remote(0, 2, 0, 2)
    near = remote(0, 1, 0, 1)
    relay = remote(0, 1, 2, 3)
    small = [remote(i, k, 0, k) for k in (2, 3, 1) for i in range(1, n_arr)]
    far.start()
    near.start()
    for cp in small:
        cp.start()
    far.wait_recv()
    relay.start()
    near.wait()
    for cp in small:
        cp.wait()
    far.wait_send()
    relay.wait()


def gather_homes(arrays, n_dev):
    outs = [jax.ShapeDtypeStruct((n_dev,) + a.shape, a.dtype) for a in arrays]
    return pl.pallas_call(
        functools.partial(gather_kernel, n_dev),
        out_shape=outs,
        in_specs=[pl.BlockSpec(memory_space=pl.ANY)] * len(arrays),
        out_specs=[pl.BlockSpec(memory_space=pltpu.VMEM)] * len(arrays),
        scratch_shapes=[
            pltpu.SemaphoreType.DMA((len(arrays),)),
            pltpu.SemaphoreType.DMA((len(arrays), n_dev)),
            pltpu.SemaphoreType.DMA((len(arrays), n_dev)),
        ],
        compiler_params=pltpu.CompilerParams(collective_id=0, has_side_effects=True),
        name="gather_homes",
    )(*arrays)


def dot(a, b, ca, cb):
    return lax.dot_general(a, b, (((ca,), (cb,)), ((), ())), preferred_element_type=F32)


def expert_kernel(n_dev, cap, cnt_ref, gy_ref, tk_ref, sl_ref, gt_ref, hg_ref, hu_ref, wg_ref, wu_ref, wd_ref,
                  dwd_ref, dh1_ref, dh3_ref, *rest):
    part_refs = rest[:n_dev]
    key_ref, gate_ref, part_acc = rest[n_dev:]
    e = pl.program_id(0)
    n_loc = pl.num_programs(0)
    me = lax.axis_index("ep")
    expert = me * n_loc + e
    tok = sl_ref.shape[2]
    rows = n_dev * cap
    cols = n_dev * tok

    @pl.when(e == 0)
    def _():
        keys = [jnp.where(sl_ref[k] >= 0, tk_ref[k] * cap + sl_ref[k], -1) for k in range(n_dev)]
        key_ref[...] = jnp.concatenate(keys, axis=1)
        gate_ref[...] = jnp.concatenate([gt_ref[k] for k in range(n_dev)], axis=1)
        part_acc[...] = jnp.zeros_like(part_acc)

    row_id = lax.broadcasted_iota(jnp.int32, (rows, cols), 0)
    col_id = lax.broadcasted_iota(jnp.int32, (rows, cols), 1)
    target = jnp.where(((row_id // cap) ^ me) == col_id // tok, expert * cap + row_id % cap, -2)
    gate_sel = jnp.zeros((rows, cols), F32)
    pick = jnp.zeros((rows, cols), F32)
    for j in range(key_ref.shape[0]):
        hit = key_ref[j:j + 1, :] == target
        gate_sel = jnp.where(hit, gate_ref[j:j + 1, :], gate_sel)
        pick = jnp.where(hit, 1.0, pick)
    pick = pick.astype(BF16)
    row_gate = jnp.sum(gate_sel, axis=1, keepdims=True)
    row1 = lax.broadcasted_iota(jnp.int32, (rows, 1), 0)
    count = jnp.zeros((rows, 1), jnp.int32)
    for s in range(n_dev):
        count = jnp.where(row1 // cap == s, cnt_ref[s ^ me, expert], count)
    keep = row1 % cap < count
    gy_all = gy_ref[...].reshape(cols, gy_ref.shape[2])
    gated = dot(pick, gy_all, 1, 0) * row_gate
    grad_rows = jnp.where(keep, gated, 0.0).astype(BF16)

    gate_f = hg_ref[0].astype(F32)
    up_f = hu_ref[0].astype(F32)
    gate_sig = jax.nn.sigmoid(gate_f)
    gate_act = gate_f * gate_sig
    hidden_act = (gate_act * up_f).astype(BF16)
    grad_h = dot(grad_rows, wd_ref[0], 1, 1).astype(BF16).astype(F32)
    grad_hgate = (grad_h * up_f * gate_sig * (1.0 + gate_f * (1.0 - gate_sig))).astype(BF16)
    grad_hup = (grad_h * gate_act).astype(BF16)
    dh1_ref[0] = grad_hgate
    dh3_ref[0] = grad_hup
    dwd_ref[0] = dot(hidden_act, grad_rows, 0, 0)
    ret = (dot(grad_hgate, wg_ref[0], 1, 1) + dot(grad_hup, wu_ref[0], 1, 1)).astype(BF16)
    part_acc[...] += dot(pick, ret, 0, 0)

    @pl.when(e == n_loc - 1)
    def _():
        for k in range(n_dev):
            part_refs[k][...] = part_acc[k * tok:(k + 1) * tok, :]


def expert_pass(counts, gy, tk, sl, gt, hg, hu, wg, wu, wd, n_dev, cap):
    n_loc, ffn, model = wd.shape
    rows = hg.shape[1]
    tok = gy.shape[1]
    top_k = tk.shape[1]
    whole = lambda a: pl.BlockSpec(a.shape, lambda e: (0,) * a.ndim)
    per_e = lambda a: pl.BlockSpec((1,) + a.shape[1:], lambda e: (e, 0, 0))
    out_shape = [
        jax.ShapeDtypeStruct((n_loc, ffn, model), F32),
        jax.ShapeDtypeStruct((n_loc, rows, ffn), BF16),
        jax.ShapeDtypeStruct((n_loc, rows, ffn), BF16),
    ] + [jax.ShapeDtypeStruct((tok, model), F32)] * n_dev
    return pl.pallas_call(
        functools.partial(expert_kernel, n_dev, cap),
        grid=(n_loc,),
        out_shape=out_shape,
        in_specs=[pl.BlockSpec(memory_space=pltpu.SMEM), whole(gy), whole(tk), whole(sl), whole(gt),
                  per_e(hg), per_e(hu), per_e(wg), per_e(wu), per_e(wd)],
        out_specs=[per_e(out_shape[0]), per_e(out_shape[1]), per_e(out_shape[2])]
        + [pl.BlockSpec((tok, model), lambda e: (0, 0))] * n_dev,
        scratch_shapes=[
            pltpu.VMEM((top_k, n_dev * tok), jnp.int32),
            pltpu.VMEM((top_k, n_dev * tok), F32),
            pltpu.VMEM((n_dev * tok, model), F32),
        ],
        compiler_params=pltpu.CompilerParams(dimension_semantics=("arbitrary",), vmem_limit_bytes=48 * 2**20),
        cost_estimate=pl.CostEstimate(flops=10 * n_loc * rows * ffn * model, bytes_accessed=50 * 2**20, transcendentals=0),
        name="expert_pass",
    )(counts, gy, tk, sl, gt, hg, hu, wg, wu, wd)


def weight_kernel(x_ref, dh1_ref, dh3_ref, gy_ref, y_ref, dwg_ref, dwu_ref, gg_ref, gg_acc):
    e = pl.program_id(0)
    x = x_ref[0]
    dwg_ref[0] = dot(x, dh1_ref[0], 0, 0)
    dwu_ref[0] = dot(x, dh3_ref[0], 0, 0)
    prod = y_ref[...].astype(F32) * gy_ref[...].astype(F32)[:, None, :]
    step = y_ref.shape[0]
    gg_acc[pl.ds(pl.multiple_of(e * step, step), step), 0:y_ref.shape[1]] = jnp.sum(prod, axis=2)

    @pl.when(e == pl.num_programs(0) - 1)
    def _():
        gg_ref[...] = gg_acc[...].T[0:y_ref.shape[1], :]


def weight_pass(x, dh1, dh3, gy, y):
    n_loc, rows, model = x.shape
    ffn = dh1.shape[2]
    tok, top_k, _ = y.shape
    step = tok // n_loc
    per_e = lambda shape: pl.BlockSpec((1,) + shape[1:], lambda e: (e, 0, 0))
    grad_shape = jax.ShapeDtypeStruct((n_loc, model, ffn), F32)
    return pl.pallas_call(
        weight_kernel,
        grid=(n_loc,),
        out_shape=[grad_shape, grad_shape, jax.ShapeDtypeStruct((top_k, tok), F32)],
        in_specs=[per_e(x.shape), per_e(dh1.shape), per_e(dh3.shape),
                  pl.BlockSpec((step, model), lambda e: (e, 0)),
                  pl.BlockSpec((step, top_k, model), lambda e: (e, 0, 0))],
        out_specs=[per_e(grad_shape.shape), per_e(grad_shape.shape), pl.BlockSpec((top_k, tok), lambda e: (0, 0))],
        scratch_shapes=[pltpu.VMEM((tok, 128), F32)],
        compiler_params=pltpu.CompilerParams(dimension_semantics=("arbitrary",), vmem_limit_bytes=40 * 2**20),
        cost_estimate=pl.CostEstimate(flops=4 * n_loc * rows * ffn * model, bytes_accessed=40 * 2**20, transcendentals=0),
        name="weight_pass",
    )(x, dh1, dh3, gy, y)


def solution(mesh):
    n_dev = mesh.shape["ep"]
    rows_spec = P(("dp", "ep"), None)
    cube_spec = P(("dp", "ep"), None, None)
    weight_spec = P("ep", None, None)

    def local_step(grad_y, gate_vals, topk_idx, slot_ids, pair_counts, y_routed, x_disp, h_gate, h_up, w_gate, w_up, w_down):
        cap = x_disp.shape[1] // n_dev
        gy, tk, sl, gt, ct = gather_homes([grad_y, topk_idx.T, slot_ids.T, gate_vals.T, pair_counts], n_dev)
        dwd, dh1, dh3, *parts = expert_pass(ct[:, 0, :], gy, tk, sl, gt, h_gate, h_up, w_gate, w_up, w_down, n_dev, cap)
        back = [lax.ppermute(parts[k], "ep", [(i, i ^ k) for i in range(n_dev)]) for k in range(1, n_dev)]
        dwg, dwu, gg = weight_pass(x_disp, dh1, dh3, grad_y, y_routed)
        total = parts[0]
        for b in back:
            total = total + b
        return total.astype(BF16), gg.T, dwg, dwu, dwd

    return jax.shard_map(local_step, mesh=mesh, in_specs=(rows_spec, rows_spec, rows_spec, rows_spec, rows_spec, cube_spec, cube_spec, cube_spec, cube_spec, weight_spec, weight_spec, weight_spec), out_specs=(rows_spec, rows_spec, cube_spec, cube_spec, cube_spec), check_vma=False)
```

time: 158 us -> 53.8 us (0.34)
  local copies, waits for them, and re-layouts: 60.2 us -> 6.31 us
  matrix products: 52.5 us -> 0 us
  Pallas kernels: 0 us -> 43.8 us
  waiting for transfers between devices: 22.3 us -> 0.01 us
  starting transfers between devices: 13.6 us -> 1.86 us
  other arithmetic: 6.9 us -> 0.73 us
    dot_general x7 -> x0, matrix products: 52.5 us -> none  [the longest x1 10.5 us: expert_grads(): jnp.einsum('erf,erd->efd', hidden_act, grad_rows, preferred_element_type=...]
    pallas_call x0 -> x3, Pallas kernels: none -> 43.8 us  [the longest x1 21.5 us: expert_pass(): pl.pallas_call(functools.partial(expert_kernel, n_dev, cap), grid=(n_loc,...]
    unnamed x20, local copies, waits for them, and re-layouts: 35.5 us -> 6.31 us
    all_to_all x3 -> x0, waiting for transfers between devices: 22.3 us -> none  [the longest x1 22.3 us: local_step(): lax.all_to_all(send_rows.reshape(n_dev, n_loc, cap_rows, model_dim), 'ep'...]
    gather x3 -> x0, local copies, waits for them, and re-layouts: 16.8 us -> none  [the longest x1 6.87 us: build_send(): jnp.take(gate_vals.reshape(-1), row_source, mode='fill', fill_value=0)]
    all_to_all x3 -> x0, starting transfers between devices: 13.6 us -> none  [the longest x1 4.62 us: local_step(): lax.all_to_all(grad_disp.reshape(n_loc, n_dev, cap_rows, model_dim), 'ep'...]
    convert_element_type x1, other arithmetic: 3.49 us -> 0.73 us  [local_step(): return (total.astype(BF16), gg.T, dwg, dwu, dwd)]
    scatter x1 -> x0, local copies, waits for them, and re-layouts: 2.45 us -> none  [build_send(): jnp.full((n_exp * cap_rows,), tok_dev * top_k, jnp.int32).at[dest_row]]
  transfers between devices with their start and end apart: 3 -> 3, of which waited for: 1 -> 0; matrix products, arithmetic and copies ran while one was open for 55% -> 0% of each run, Pallas kernels for 0% -> 23%
where the time goes in v1:
time: 53.8 us; the launch traced here: 53.3 us
  Pallas kernels  43.8 us (81%)
  local copies, waits for them, and re-layouts  6.31 us (12%)
  starting transfers between devices  1.86 us (3%)
  other arithmetic  0.73 us (1%)
  between operations  0.67 us (1%)
    pallas_call x1, Pallas kernels, expert_pass(): pl.pallas_call(functools.partial(expert_kernel, n_dev, cap), grid=(n_loc,...  21.5 us
    pallas_call x1, Pallas kernels, weight_pass(): pl.pallas_call(weight_kernel, grid=(n_loc,), out_shape=[grad_shape, grad_...  12.2 us
    pallas_call x1, Pallas kernels, gather_homes(): pl.pallas_call(functools.partial(gather_kernel, n_dev), out_shape=outs, i...  10.1 us
    unnamed x20, local copies, waits for them, and re-layouts  6.31 us
    ppermute x3, starting transfers between devices, local_step(): lax.ppermute(parts[k], 'ep', [(i, i ^ k) for i in range(n_dev)])  1.86 us
  transfers between devices with their start and end apart: 3, of which 0 were waited for; matrix products, arithmetic and copies ran while one was open for 0% of the time, Pallas kernels for 23%

profile of v1, /device:TPU:0, one launch (start us, length us, event | category | flops | bytes accessed | tf_op | source)
XLA Modules:
  0.0 53.3 jit_solution(10414227178935697423)
XLA Ops:
  0.6 10.1 %gather_homes.1 = (bf16[4,64,1024]{2,1,0:T(8,128)(2,1)}, s32[4,8,64]{2,1,0:T(8,128)}, s32[4,8,64]{2,1,0:T(8,128)}, f32[4,8,64]{2,1,0:T(8,128)}, s32[4,1,32]{2,1,0:T(1,128)}) custom-call(bf16[64,1024]{1,0:T(8,128)(2,1)} %gy_ref.1, s32[8,64]{1,0:T(8,128)} %bitcast.6, s32[8,64]{1,0:T(8,128)} %bitcast.7, f32[8,64]{1,0:T(8,128)} %bitcast.8, s32[1,32]{1,0:T(1,128)} %refs_4_.1), custom_call_target="tpu_custom_call" | custom-call | tf_op jit(solution)/shard_map/gather_homes/pallas_call | solution.py:55
  10.8 0.0 copy-start
  10.8 1.2 %copy-done = bf16[8,128,512]{2,1,0:T(8,128)(2,1)S(1)} copy-done((bf16[8,128,512]{2,1,0:T(8,128)(2,1)S(1)}, bf16[8,128,512]{2,1,0:T(8,128)(2,1)}, u32[]{:S(2)}) %copy-start) | copy-done | bytes 1048600
  12.0 0.0 copy-start.1
  12.0 1.2 %copy-done.1 = bf16[8,128,512]{2,1,0:T(8,128)(2,1)S(1)} copy-done((bf16[8,128,512]{2,1,0:T(8,128)(2,1)S(1)}, bf16[8,128,512]{2,1,0:T(8,128)(2,1)}, u32[]{:S(2)}) %copy-start.1) | copy-done | bytes 1048600
  13.2 0.0 copy-start.2
  13.2 1.0 %copy-done.2 = bf16[4,64,1024]{2,1,0:T(8,128)(2,1)S(1)} copy-done((bf16[4,64,1024]{2,1,0:T(8,128)(2,1)S(1)}, bf16[4,64,1024]{2,1,0:T(8,128)(2,1)}, u32[]{:S(2)}) %copy-start.2) | copy-done | bytes 524312
  14.3 0.0 copy-start.4
  14.3 0.7 %copy-done.4 = s32[4,8,64]{2,1,0:T(8,128)S(1)} copy-done((s32[4,8,64]{2,1,0:T(8,128)S(1)}, s32[4,8,64]{2,1,0:T(8,128)}, u32[]{:S(2)}) %copy-start.4) | copy-done | bytes 8216
  15.0 0.7 %copy-done.5 = s32[4,8,64]{2,1,0:T(8,128)S(1)} copy-done((s32[4,8,64]{2,1,0:T(8,128)S(1)}, s32[4,8,64]{2,1,0:T(8,128)}, u32[]{:S(2)}) %copy-start.5) | copy-done | bytes 8216
  15.7 0.7 %copy-done.6 = f32[4,8,64]{2,1,0:T(8,128)S(1)} copy-done((f32[4,8,64]{2,1,0:T(8,128)S(1)}, f32[4,8,64]{2,1,0:T(8,128)}, u32[]{:S(2)}) %copy-start.6) | copy-done | bytes 8216
  16.4 0.7 %copy-done.7 = s32[4,1,32]{2,1,0:T(1,128)S(1)} copy-done((s32[4,1,32]{2,1,0:T(1,128)S(1)}, s32[4,1,32]{2,1,0:T(1,128)}, u32[]{:S(2)}) %copy-start.7) | copy-done | bytes 536
  17.1 21.5 %expert_pass.1 = (f32[8,512,1024]{2,1,0:T(8,128)}, bf16[8,128,512]{2,1,0:T(8,128)(2,1)S(1)}, bf16[8,128,512]{2,1,0:T(8,128)(2,1)S(1)}, f32[64,1024]{1,0:T(8,128)...) custom-call(s32[4,32]{1,0:T(4,128)S(1)} %bitcast.5, ...), custom_call_target="tpu_custom_call" | custom-call | flops 5368709120 | bytes 52428800 | tf_op jit(solution)/shard_map/expert_pass/pallas_call | solution.py:145
  38.5 0.4 collective-permute-start
  38.9 1.4 %collective-permute-start.1 = (f32[64,1024]{1,0:T(8,128)S(1)}, f32[64,1024]{1,0:T(8,128)S(1)}, u32[]{:S(2)}, u32[]{:S(2)}) collective-permute-start(f32[64,1024]{1,0:T(8,128)S(1)} %get-tuple-element.27), channel_id=1, source_target_pairs={{0,2},{1,3},{2,0},{3,1},{4,6},{5,7},{6,4},{7,5},{8,10},{9,11},{10,... | collective-permute-start | bytes 786440 | tf_op jit(solution)/shard_map/ppermute | solution.py:210
  40.3 0.1 collective-permute-start.2
  40.4 0.0 copy-done.3
  40.4 0.0 copy-done.8
  40.4 0.0 copy-done.9
  40.4 12.2 %weight_pass.1 = (f32[8,1024,512]{2,1,0:T(8,128)}, f32[8,1024,512]{2,1,0:T(8,128)}, f32[8,64]{1,0:T(8,128)}) custom-call(bf16[8,128,1024]{2,1,0:T(8,128)(2,1)S(1)} %copy-done.8, bf16[8,128,512]{2,1,0:T(8,128)(2,1)S(1)} %get-tuple-element.29.dh1_ref, bf16[8,128,512]{2,1,0:T(8,128)(2,1)S(1)} %get-tuple-element.30.dh3_ref, bf16[64,1024]{1,0:T(8,128)(2,1)S(1)} %copy-done.3, ...), custom_call_target="tpu_custom_call" | custom-call | flops 2147483648 | bytes 41943040 | tf_op jit(solution)/shard_map/weight_pass/pallas_call | solution.py:185
  52.6 0.0 collective-permute-done
  52.6 0.0 collective-permute-done.1
  52.6 0.0 collective-permute-done.2
  52.6 0.7 %add_convert_fusion = bf16[64,1024]{1,0:T(8,128)(2,1)} fusion(f32[64,1024]{1,0:T(8,128)S(1)} %collective-permute-done.2, f32[64,1024]{1,0:T(8,128)S(1)} %collective-permute-done.1, f32[64,1024]{1,0:T(8,128)S(1)} %get-tuple-element.25, f32[64,1024]{1,0:T(8,128)S(1)} %collective-permute-done), kind=kLoop, calls=%fused_computation | loop fusion | flops 262144 | bytes 1179648 | tf_op jit(solution)/shard_map/convert_element_type | solution.py:215
  (6 shorter events, 0.0 us)
Async XLA Ops:
  10.8 1.2 %copy-start = (bf16[8,128,512]{2,1,0:T(8,128)(2,1)S(1)}, bf16[8,128,512]{2,1,0:T(8,128)(2,1)}, u32[]{:S(2)}) copy-start(bf16[8,128,512]{2,1,0:T(8,128)(2,1)} %hg_ref.1) | copy-start | bytes 3145732
  12.0 1.2 %copy-start.1 = (bf16[8,128,512]{2,1,0:T(8,128)(2,1)S(1)}, bf16[8,128,512]{2,1,0:T(8,128)(2,1)}, u32[]{:S(2)}) copy-start(bf16[8,128,512]{2,1,0:T(8,128)(2,1)} %hu_ref.1) | copy-start | bytes 3145732
  13.2 1.0 %copy-start.2 = (bf16[4,64,1024]{2,1,0:T(8,128)(2,1)S(1)}, bf16[4,64,1024]{2,1,0:T(8,128)(2,1)}, u32[]{:S(2)}) copy-start(bf16[4,64,1024]{2,1,0:T(8,128)(2,1)} %get-tuple-element.21.gy_ref) | copy-start | bytes 1572868
  14.3 0.7 %copy-start.4 = (s32[4,8,64]{2,1,0:T(8,128)S(1)}, s32[4,8,64]{2,1,0:T(8,128)}, u32[]{:S(2)}) copy-start(s32[4,8,64]{2,1,0:T(8,128)} %get-tuple-element.22.tk_ref) | copy-start | bytes 24580
  15.0 0.7 %copy-start.5 = (s32[4,8,64]{2,1,0:T(8,128)S(1)}, s32[4,8,64]{2,1,0:T(8,128)}, u32[]{:S(2)}) copy-start(s32[4,8,64]{2,1,0:T(8,128)} %get-tuple-element.23.sl_ref) | copy-start | bytes 24580
  15.7 0.7 %copy-start.6 = (f32[4,8,64]{2,1,0:T(8,128)S(1)}, f32[4,8,64]{2,1,0:T(8,128)}, u32[]{:S(2)}) copy-start(f32[4,8,64]{2,1,0:T(8,128)} %get-tuple-element.24.gt_ref) | copy-start | bytes 24580
  16.4 0.7 %copy-start.7 = (s32[4,1,32]{2,1,0:T(1,128)S(1)}, s32[4,1,32]{2,1,0:T(1,128)}, u32[]{:S(2)}) copy-start(s32[4,1,32]{2,1,0:T(1,128)} %get-tuple-element.20) | copy-start | bytes 1540
  17.1 23.3 %copy-start.3 = (bf16[64,1024]{1,0:T(8,128)(2,1)S(1)}, bf16[64,1024]{1,0:T(8,128)(2,1)}, u32[]{:S(2)}) copy-start(bf16[64,1024]{1,0:T(8,128)(2,1)} %gy_ref.1) | copy-start | bytes 393220
  17.1 23.3 %copy-start.8 = (bf16[8,128,1024]{2,1,0:T(8,128)(2,1)S(1)}, bf16[8,128,1024]{2,1,0:T(8,128)(2,1)}, u32[]{:S(2)}) copy-start(bf16[8,128,1024]{2,1,0:T(8,128)(2,1)} %x_ref.1) | copy-start | bytes 6291460
  17.1 23.3 %copy-start.9 = (bf16[64,8,1024]{2,1,0:T(8,128)(2,1)S(1)}, bf16[64,8,1024]{2,1,0:T(8,128)(2,1)}, u32[]{:S(2)}) copy-start(bf16[64,8,1024]{2,1,0:T(8,128)(2,1)} %y_ref.1) | copy-start | bytes 3145732
  38.5 14.0 %collective-permute-start = (f32[64,1024]{1,0:T(8,128)S(1)}, f32[64,1024]{1,0:T(8,128)S(1)}, u32[]{:S(2)}, u32[]{:S(2)}) collective-permute-start(f32[64,1024]{1,0:T(8,128)S(1)} %get-tuple-element.26), channel_id=1, source_target_pairs={{0,1},{1,0},{2,3},{3,2},{4,5},{5,4},{6,7},{7,6},{8,9},{9,8},{10,11... | collective-permute-start | bytes 786440 | tf_op jit(solution)/shard_map/ppermute | solution.py:210
  38.9 13.7 %collective-permute-start.1 = (f32[64,1024]{1,0:T(8,128)S(1)}, f32[64,1024]{1,0:T(8,128)S(1)}, u32[]{:S(2)}, u32[]{:S(2)}) collective-permute-start(f32[64,1024]{1,0:T(8,128)S(1)} %get-tuple-element.27), channel_id=1, source_target_pairs={{0,2},{1,3},{2,0},{3,1},{4,6},{5,7},{6,4},{7,5},{8,10},{9,11},{10,... | collective-permute-start | bytes 786440 | tf_op jit(solution)/shard_map/ppermute | solution.py:210
  40.3 12.3 %collective-permute-start.2 = (f32[64,1024]{1,0:T(8,128)S(1)}, f32[64,1024]{1,0:T(8,128)S(1)}, u32[]{:S(2)}, u32[]{:S(2)}) collective-permute-start(f32[64,1024]{1,0:T(8,128)S(1)} %get-tuple-element.28), channel_id=1, source_target_pairs={{0,3},{1,2},{2,1},{3,0},{4,7},{5,6},{6,5},{7,4},{8,11},{9,10},{10,... | collective-permute-start | bytes 786440 | tf_op jit(solution)/shard_map/ppermute | solution.py:210

commit v2 on v1

v2 whole, which is shorter than its diff:
```python
import functools

import jax
import jax.numpy as jnp
from jax import lax
from jax.experimental import pallas as pl
from jax.experimental.pallas import tpu as pltpu
from jax.sharding import PartitionSpec as P

MESH = pl.DeviceIdType.MESH
F32 = jnp.float32
BF16 = jnp.bfloat16
ANY = pl.BlockSpec(memory_space=pl.ANY)
VMEM = pl.BlockSpec(memory_space=pltpu.VMEM)
MIB = 2**20


def dot(a, b, ca, cb):
    return lax.dot_general(a, b, (((ca,), (cb,)), ((), ())), preferred_element_type=F32)


def front_kernel(n_dev, n_tab, n_load, *refs):
    n_in = n_tab + n_load
    ins, outs = refs[:n_in], refs[n_in:2 * n_in]
    local_sem, send_sem, recv_sem = refs[2 * n_in:]
    me = lax.axis_index("ep")
    local = [pltpu.make_async_copy(ins[i], outs[i].at[0], local_sem.at[i]) for i in range(n_tab)]
    loads = [pltpu.make_async_copy(ins[i], outs[i], local_sem.at[i]) for i in range(n_tab, n_in)]
    for cp in local:
        cp.start()
    barrier = pltpu.get_barrier_semaphore()
    for k in range(1, n_dev):
        pl.semaphore_signal(barrier, inc=1, device_id={"ep": me ^ k}, device_id_type=MESH)
    for cp in loads:
        cp.start()
    pl.semaphore_wait(barrier, n_dev - 1)
    for cp in local:
        cp.wait()

    def remote(i, k, src_slot, dst_slot):
        return pltpu.make_async_remote_copy(
            src_ref=outs[i].at[src_slot], dst_ref=outs[i].at[dst_slot],
            send_sem=send_sem.at[i, dst_slot], recv_sem=recv_sem.at[i, dst_slot],
            device_id={"ep": me ^ k}, device_id_type=MESH)

    far = remote(0, 2, 0, 2)
    near = remote(0, 1, 0, 1)
    relay = remote(0, 1, 2, 3)
    small = [remote(i, k, 0, k) for k in (2, 3, 1) for i in range(1, n_tab)]
    far.start()
    near.start()
    for cp in small:
        cp.start()
    far.wait_recv()
    relay.start()
    near.wait()
    for cp in small:
        cp.wait()
    far.wait_send()
    relay.wait()
    for cp in loads:
        cp.wait()


def front_pass(tables, loads, n_dev):
    outs = [pltpu.VMEM((n_dev,) + a.shape, a.dtype) for a in tables] + [pltpu.VMEM(a.shape, a.dtype) for a in loads]
    n_in = len(outs)
    return pl.pallas_call(
        functools.partial(front_kernel, n_dev, len(tables), len(loads)),
        out_shape=outs,
        in_specs=[ANY] * n_in,
        out_specs=[VMEM] * n_in,
        scratch_shapes=[
            pltpu.SemaphoreType.DMA((n_in,)),
            pltpu.SemaphoreType.DMA((len(tables), n_dev)),
            pltpu.SemaphoreType.DMA((len(tables), n_dev)),
        ],
        compiler_params=pltpu.CompilerParams(collective_id=0, has_side_effects=True, vmem_limit_bytes=4 * MIB),
        name="front_pass",
    )(*[pltpu.with_memory_space_constraint(a, pltpu.HBM) for a in (*tables, *loads)])


def expert_kernel(n_dev, cap, gy_ref, tk_ref, sl_ref, gt_ref, ct_ref, hg_ref, hu_ref, wg_ref, wu_ref, wd_ref,
                  dwd_ref, dh1_ref, dh3_ref, *rest):
    part_refs = rest[:n_dev]
    key_ref, gate_ref = rest[n_dev:n_dev + 2]
    slots = [rest[n_dev + 2 + 6 * s:n_dev + 8 + 6 * s] for s in range(2)]
    out_sem = rest[n_dev + 14]
    n_loc = wd_ref.shape[0]
    me = lax.axis_index("ep")
    tok = sl_ref.shape[2]
    rows = n_dev * cap
    cols = n_dev * tok

    keys = [jnp.where(sl_ref[k] >= 0, tk_ref[k] * cap + sl_ref[k], -1) for k in range(n_dev)]
    key_ref[...] = jnp.concatenate(keys, axis=1)
    gate_ref[...] = jnp.concatenate([gt_ref[k] for k in range(n_dev)], axis=1)
    for k in range(n_dev):
        part_refs[k][...] = jnp.zeros_like(part_refs[k])

    def out_copy(e, s):
        return pltpu.make_async_copy(slots[s][5], dwd_ref.at[e], out_sem.at[s])

    def front(e, s):
        pick_s, act_s, grad_s, dh1_s, dh3_s, _ = slots[s]
        expert = me * n_loc + e
        row_id = lax.broadcasted_iota(jnp.int32, (rows, cols), 0)
        col_id = lax.broadcasted_iota(jnp.int32, (rows, cols), 1)
        target = jnp.where(((row_id // cap) ^ me) == col_id // tok, expert * cap + row_id % cap, -2)
        gate_sel = jnp.zeros((rows, cols), F32)
        pick = jnp.zeros((rows, cols), F32)
        for j in range(key_ref.shape[0]):
            hit = key_ref[j:j + 1, :] == target
            gate_sel = jnp.where(hit, gate_ref[j:j + 1, :], gate_sel)
            pick = jnp.where(hit, 1.0, pick)
        pick = pick.astype(BF16)
        row_gate = jnp.sum(gate_sel, axis=1, keepdims=True)
        row1 = lax.broadcasted_iota(jnp.int32, (rows, 1), 0)
        lane = lax.broadcasted_iota(jnp.int32, ct_ref.shape[1:], 1)
        count = jnp.zeros((rows, 1), jnp.int32)
        for k in range(n_dev):
            here = jnp.sum(jnp.where(lane == expert, ct_ref[k], 0), axis=1, keepdims=True)
            count = jnp.where((row1 // cap) ^ me == k, here, count)
        gated = dot(pick, gy_ref[...].reshape(cols, gy_ref.shape[2]), 1, 0) * row_gate
        grad_rows = jnp.where(row1 % cap < count, gated, 0.0).astype(BF16)
        gate_f = hg_ref[e].astype(F32)
        up_f = hu_ref[e].astype(F32)
        gate_sig = jax.nn.sigmoid(gate_f)
        gate_act = gate_f * gate_sig
        grad_h = dot(grad_rows, wd_ref[e], 1, 1).astype(BF16).astype(F32)
        grad_hgate = (grad_h * up_f * gate_sig * (1.0 + gate_f * (1.0 - gate_sig))).astype(BF16)
        grad_hup = (grad_h * gate_act).astype(BF16)
        pick_s[...] = pick
        act_s[...] = (gate_act * up_f).astype(BF16)
        grad_s[...] = grad_rows
        dh1_s[...] = grad_hgate
        dh3_s[...] = grad_hup
        dh1_ref[e] = grad_hgate
        dh3_ref[e] = grad_hup

    def back(e, s):
        pick_s, act_s, grad_s, dh1_s, dh3_s, stage = slots[s]
        ret = (dot(dh1_s[...], wg_ref[e], 1, 1) + dot(dh3_s[...], wu_ref[e], 1, 1)).astype(BF16)
        part = dot(pick_s[...], ret, 0, 0)
        for k in range(n_dev):
            part_refs[k][...] += part[k * tok:(k + 1) * tok, :]
        stage[...] = dot(act_s[...], grad_s[...], 0, 0)
        out_copy(e, s).start()

    def pair(i, last):
        e = 2 * i

        @pl.when(i > 0)
        def _():
            out_copy(e, 0).wait()

        front(e + 1, 1)
        back(e, 0)

        @pl.when(i > 0)
        def _():
            out_copy(e, 1).wait()

        if not last:
            front(e + 2, 0)
        back(e + 1, 1)

    front(0, 0)

    def body(i, carry):
        pair(i, False)
        return carry

    lax.fori_loop(0, n_loc // 2 - 1, body, 0)
    pair(n_loc // 2 - 1, True)
    out_copy(0, 0).wait()
    out_copy(0, 1).wait()


def expert_pass(gy, tk, sl, gt, ct, hg, hu, wg, wu, wd, n_dev, cap):
    n_loc, ffn, model = wd.shape
    rows = hg.shape[1]
    tok = gy.shape[1]
    top_k = tk.shape[1]
    slot = [
        pltpu.VMEM((rows, n_dev * tok), BF16),
        pltpu.VMEM((rows, ffn), BF16),
        pltpu.VMEM((rows, model), BF16),
        pltpu.VMEM((rows, ffn), BF16),
        pltpu.VMEM((rows, ffn), BF16),
        pltpu.VMEM((ffn, model), F32),
    ]
    return pl.pallas_call(
        functools.partial(expert_kernel, n_dev, cap),
        out_shape=[
            jax.ShapeDtypeStruct((n_loc, ffn, model), F32),
            pltpu.VMEM((n_loc, rows, ffn), BF16),
            pltpu.VMEM((n_loc, rows, ffn), BF16),
        ] + [pltpu.VMEM((tok, model), F32)] * n_dev,
        in_specs=[VMEM] * 10,
        out_specs=[ANY, VMEM, VMEM] + [VMEM] * n_dev,
        scratch_shapes=[
            pltpu.VMEM((top_k, n_dev * tok), jnp.int32),
            pltpu.VMEM((top_k, n_dev * tok), F32),
        ] + slot + slot + [pltpu.SemaphoreType.DMA((2,))],
        compiler_params=pltpu.CompilerParams(vmem_limit_bytes=EXPERT_VMEM),
        cost_estimate=pl.CostEstimate(flops=10 * n_loc * rows * ffn * model, bytes_accessed=50 * MIB, transcendentals=0),
        name="expert_pass",
    )(gy, tk, sl, gt, ct, hg, hu, wg, wu, wd)


EXPERT_VMEM = 14 * MIB
WEIGHT_VMEM = 20 * MIB


def weight_kernel(x_ref, dh1_ref, dh3_ref, gy_ref, y_ref, dwg_ref, dwu_ref, gg_ref, stage, gg_acc, out_sem, gg_sem):
    n_loc, _, model = x_ref.shape
    top_k = y_ref.shape[1]
    half = model // 2

    def out_copy(e, s, q):
        dst = (dwg_ref, dwu_ref)[q % 2].at[e, pl.ds(half * (q // 2), half), :]
        return pltpu.make_async_copy(stage.at[s, q], dst, out_sem.at[s, q])

    def one(e, s):
        for h in range(2):
            x = x_ref[e, :, h * half:(h + 1) * half]
            for w, dh in enumerate((dh1_ref, dh3_ref)):
                q = 2 * h + w
                stage[s, q] = dot(x, dh[e], 0, 0)
                out_copy(e, s, q).start()

    def wait_all(s):
        for q in range(4):
            out_copy(0, s, q).wait()

    def body(i, carry):
        for s in range(2):
            @pl.when(i > 0)
            def _():
                wait_all(s)
            one(2 * i + s, s)

        @pl.when(i == n_loc // 2 - 2)
        def _():
            step = 8
            for b in range(y_ref.shape[0] // step):
                prod = y_ref[b * step:(b + 1) * step].astype(F32) * gy_ref[0, b * step:(b + 1) * step].astype(F32)[:, None, :]
                gg_acc[b * step:(b + 1) * step, 0:top_k] = jnp.sum(prod, axis=2)
            gg_ref[...] = gg_acc[...].T[0:top_k, :]
        return carry

    lax.fori_loop(0, n_loc // 2, body, 0)
    wait_all(0)
    wait_all(1)


def weight_pass(x, dh1, dh3, gy, y):
    n_loc, rows, model = x.shape
    ffn = dh1.shape[2]
    tok, top_k, _ = y.shape
    grad_shape = jax.ShapeDtypeStruct((n_loc, model, ffn), F32)
    return pl.pallas_call(
        weight_kernel,
        out_shape=[grad_shape, grad_shape, jax.ShapeDtypeStruct((top_k, tok), F32)],
        in_specs=[VMEM] * 5,
        out_specs=[ANY, ANY, VMEM],
        scratch_shapes=[
            pltpu.VMEM((2, 4, model // 2, ffn), F32),
            pltpu.VMEM((tok, 128), F32),
            pltpu.SemaphoreType.DMA((2, 4)),
            pltpu.SemaphoreType.DMA,
        ],
        compiler_params=pltpu.CompilerParams(vmem_limit_bytes=WEIGHT_VMEM),
        cost_estimate=pl.CostEstimate(flops=4 * n_loc * rows * ffn * model, bytes_accessed=40 * MIB, transcendentals=0),
        name="weight_pass",
    )(x, dh1, dh3, gy, y)


def solution(mesh):
    n_dev = mesh.shape["ep"]
    rows_spec = P(("dp", "ep"), None)
    cube_spec = P(("dp", "ep"), None, None)
    weight_spec = P("ep", None, None)

    def local_step(grad_y, gate_vals, topk_idx, slot_ids, pair_counts, y_routed, x_disp, h_gate, h_up, w_gate, w_up, w_down):
        cap = x_disp.shape[1] // n_dev
        tables = [grad_y, topk_idx.T, slot_ids.T, gate_vals.T, pair_counts]
        loads = [w_down, h_gate, h_up, w_gate, w_up, x_disp, y_routed]
        gy, tk, sl, gt, ct, wd, hg, hu, wg, wu, x, y = front_pass(tables, loads, n_dev)
        dwd, dh1, dh3, *parts = expert_pass(gy, tk, sl, gt, ct, hg, hu, wg, wu, wd, n_dev, cap)
        back = [lax.ppermute(parts[k], "ep", [(i, i ^ k) for i in range(n_dev)]) for k in range(1, n_dev)]
        dwg, dwu, gg = weight_pass(x, dh1, dh3, gy, y)
        total = parts[0]
        for b in back:
            total = total + b
        return total.astype(BF16), gg.T, dwg, dwu, dwd

    return jax.shard_map(local_step, mesh=mesh, in_specs=(rows_spec, rows_spec, rows_spec, rows_spec, rows_spec, cube_spec, cube_spec, cube_spec, cube_spec, weight_spec, weight_spec, weight_spec), out_specs=(rows_spec, rows_spec, cube_spec, cube_spec, cube_spec), check_vma=False)
```

time: 53.8 us -> 44.4 us (0.83)
  local copies, waits for them, and re-layouts: 6.31 us -> 0 us
  Pallas kernels: 43.8 us -> 39.2 us
  starting transfers between devices: 1.86 us -> 3.37 us
    unnamed x20 -> x0, local copies, waits for them, and re-layouts: 6.31 us -> none
    pallas_call x3, Pallas kernels: 43.8 us -> 39.2 us  [the longest x1 17.1 us: expert_pass(): pl.pallas_call(functools.partial(expert_kernel, n_dev, cap), out_shape=[j...]
    ppermute x3, starting transfers between devices: 1.86 us -> 3.37 us  [local_step(): lax.ppermute(parts[k], 'ep', [(i, i ^ k) for i in range(n_dev)])]
  transfers between devices with their start and end apart: 3 -> 3, of which waited for: 0 -> 1; matrix products, arithmetic and copies ran while one was open for 0% -> 0% of each run, Pallas kernels for 23% -> 27%
where the time goes in v2:
time: 44.4 us; the launch traced here: 44.3 us
  Pallas kernels  39.2 us (88%)
  starting transfers between devices  3.37 us (8%)
  other arithmetic  0.73 us (2%)
  between operations  0.68 us (2%)
    pallas_call x1, Pallas kernels, expert_pass(): pl.pallas_call(functools.partial(expert_kernel, n_dev, cap), out_shape=[j...  17.1 us
    pallas_call x1, Pallas kernels, weight_pass(): pl.pallas_call(weight_kernel, out_shape=[grad_shape, grad_shape, jax.Shap...  11.8 us
    pallas_call x1, Pallas kernels, front_pass(): pl.pallas_call(functools.partial(front_kernel, n_dev, len(tables), len(lo...  10.2 us
    ppermute x3, starting transfers between devices, local_step(): lax.ppermute(parts[k], 'ep', [(i, i ^ k) for i in range(n_dev)])  3.37 us
  transfers between devices with their start and end apart: 3, of which 1 were waited for; matrix products, arithmetic and copies ran while one was open for 0% of the time, Pallas kernels for 27%

profile of v2, /device:TPU:0, one launch (start us, length us, event | category | flops | bytes accessed | tf_op | source)
XLA Modules:
  0.0 44.3 jit_solution(8376700737925525295)
XLA Ops:
  0.6 10.2 %front_pass.1 = (bf16[4,64,1024]{2,1,0:T(8,128)(2,1)S(1)}, s32[4,8,64]{2,1,0:T(8,128)S(1)}, s32[4,8,64]{2,1,0:T(8,128)S(1)}, f32[4,8,64]{2,1,0:T(8,128)S(1)}, s3...) custom-call(bf16[64,1024]{1,0:T(8,128)(2,1)} %refs_0_.1, ...), custom_call_target="tpu_custom_call" | custom-call | tf_op jit(solution)/shard_map/front_pass/pallas_call | solution.py:68
  10.8 17.1 %expert_pass.1 = (f32[8,512,1024]{2,1,0:T(8,128)}, bf16[8,128,512]{2,1,0:T(8,128)(2,1)S(1)}, bf16[8,128,512]{2,1,0:T(8,128)(2,1)S(1)}, f32[64,1024]{1,0:T(8,128)...) custom-call(bf16[4,64,1024]{2,1,0:T(8,128)(2,1)S(1)} %get-tuple-element.27.gy_ref, ...), custom_call_target="tpu_custom_call" | custom-call | flops 5368709120 | bytes 52428800 | tf_op jit(solution)/shard_map/expert_pass/pallas_call | solution.py:193
  28.0 0.8 %collective-permute-start = (f32[64,1024]{1,0:T(8,128)S(1)}, f32[64,1024]{1,0:T(8,128)S(1)}, u32[]{:S(2)}, u32[]{:S(2)}) collective-permute-start(f32[64,1024]{1,0:T(8,128)S(1)} %get-tuple-element.38), channel_id=1, source_target_pairs={{0,1},{1,0},{2,3},{3,2},{4,5},{5,4},{6,7},{7,6},{8,9},{9,8},{10,11... | collective-permute-start | bytes 786440 | tf_op jit(solution)/shard_map/ppermute | solution.py:292
  28.7 2.5 %collective-permute-start.1 = (f32[64,1024]{1,0:T(8,128)S(1)}, f32[64,1024]{1,0:T(8,128)S(1)}, u32[]{:S(2)}, u32[]{:S(2)}) collective-permute-start(f32[64,1024]{1,0:T(8,128)S(1)} %get-tuple-element.39), channel_id=1, source_target_pairs={{0,2},{1,3},{2,0},{3,1},{4,6},{5,7},{6,4},{7,5},{8,10},{9,11},{10,... | collective-permute-start | bytes 786440 | tf_op jit(solution)/shard_map/ppermute | solution.py:292
  31.3 0.1 collective-permute-start.2
  31.4 11.8 %weight_pass.1 = (f32[8,1024,512]{2,1,0:T(8,128)}, f32[8,1024,512]{2,1,0:T(8,128)}, f32[8,64]{1,0:T(8,128)}) custom-call(bf16[8,128,1024]{2,1,0:T(8,128)(2,1)S(1)} %get-tuple-element.41.x_ref, bf16[8,128,512]{2,1,0:T(8,128)(2,1)S(1)} %get-tuple-element.42.dh1_ref, bf16[8,128,512]{2,1,0:T(8,128)(2,1)S(1)} %get-tuple-element.43.dh3_ref, ...), custom_call_target="tpu_custom_call" | custom-call | flops 2147483648 | bytes 41943040 | tf_op jit(solution)/shard_map/weight_pass/pallas_call | solution.py:263
  43.2 0.0 collective-permute-done
  43.2 0.0 collective-permute-done.1
  43.2 0.4 collective-permute-done.2
  43.6 0.7 %add_convert_fusion = bf16[64,1024]{1,0:T(8,128)(2,1)} fusion(f32[64,1024]{1,0:T(8,128)S(1)} %collective-permute-done.2, f32[64,1024]{1,0:T(8,128)S(1)} %collective-permute-done.1, f32[64,1024]{1,0:T(8,128)S(1)} %get-tuple-element.37, f32[64,1024]{1,0:T(8,128)S(1)} %collective-permute-done), kind=kLoop, calls=%fused_computation | loop fusion | flops 262144 | bytes 1179648 | tf_op jit(solution)/shard_map/convert_element_type | solution.py:297
Async XLA Ops:
  28.0 15.2 %collective-permute-start = (f32[64,1024]{1,0:T(8,128)S(1)}, f32[64,1024]{1,0:T(8,128)S(1)}, u32[]{:S(2)}, u32[]{:S(2)}) collective-permute-start(f32[64,1024]{1,0:T(8,128)S(1)} %get-tuple-element.38), channel_id=1, source_target_pairs={{0,1},{1,0},{2,3},{3,2},{4,5},{5,4},{6,7},{7,6},{8,9},{9,8},{10,11... | collective-permute-start | bytes 786440 | tf_op jit(solution)/shard_map/ppermute | solution.py:292
  28.7 14.5 %collective-permute-start.1 = (f32[64,1024]{1,0:T(8,128)S(1)}, f32[64,1024]{1,0:T(8,128)S(1)}, u32[]{:S(2)}, u32[]{:S(2)}) collective-permute-start(f32[64,1024]{1,0:T(8,128)S(1)} %get-tuple-element.39), channel_id=1, source_target_pairs={{0,2},{1,3},{2,0},{3,1},{4,6},{5,7},{6,4},{7,5},{8,10},{9,11},{10,... | collective-permute-start | bytes 786440 | tf_op jit(solution)/shard_map/ppermute | solution.py:292
  31.3 12.3 %collective-permute-start.2 = (f32[64,1024]{1,0:T(8,128)S(1)}, f32[64,1024]{1,0:T(8,128)S(1)}, u32[]{:S(2)}, u32[]{:S(2)}) collective-permute-start(f32[64,1024]{1,0:T(8,128)S(1)} %get-tuple-element.40), channel_id=1, source_target_pairs={{0,3},{1,2},{2,1},{3,0},{4,7},{5,6},{6,5},{7,4},{8,11},{9,10},{10,... | collective-permute-start | bytes 786440 | tf_op jit(solution)/shard_map/ppermute | solution.py:292

commit v3 on v2

v3 whole, which is shorter than its diff:
```python
import functools

import jax
import jax.numpy as jnp
from jax import lax
from jax.experimental import pallas as pl
from jax.experimental.pallas import tpu as pltpu
from jax.sharding import PartitionSpec as P

MESH = pl.DeviceIdType.MESH
F32 = jnp.float32
BF16 = jnp.bfloat16
ANY = pl.BlockSpec(memory_space=pl.ANY)
VMEM = pl.BlockSpec(memory_space=pltpu.VMEM)
MIB = 2**20
SPLIT = 4


def dot(a, b, ca, cb):
    return lax.dot_general(a, b, (((ca,), (cb,)), ((), ())), preferred_element_type=F32)


def front_kernel(n_dev, cap, gy_in, tk_in, sl_in, gt_in, ct_in, hg_in, hu_in, wd_in, wg_in, wu_in, x_in, y_in,
                 gy_ref, pick_ref, d_ref, act_ref, fac1_ref, fac3_ref, wd_ref, wg_ref, wu_ref, x_ref, y_ref,
                 tk_ref, sl_ref, gt_ref, ct_ref, hg_ref, hu_ref, gate_ref, local_sem, load_sem, send_sem, recv_sem):
    me = lax.axis_index("ep")
    n_loc = d_ref.shape[0]
    bufs = [gy_ref, tk_ref, sl_ref, gt_ref, ct_ref]
    local = [pltpu.make_async_copy(a, b.at[0], local_sem.at[i])
             for i, (a, b) in enumerate(zip((gy_in, tk_in, sl_in, gt_in, ct_in), bufs))]
    pairs = [(hg_in, hg_ref), (hu_in, hu_ref), (wd_in, wd_ref), (wg_in.at[pl.ds(0, SPLIT)], wg_ref),
             (wu_in.at[pl.ds(0, SPLIT)], wu_ref), (x_in, x_ref), (y_in, y_ref)]
    loads = [pltpu.make_async_copy(a, b, load_sem.at[i]) for i, (a, b) in enumerate(pairs)]
    for cp in local:
        cp.start()
    barrier = pltpu.get_barrier_semaphore()
    for k in range(1, n_dev):
        pl.semaphore_signal(barrier, inc=1, device_id={"ep": me ^ k}, device_id_type=MESH)
    for cp in loads:
        cp.start()
    pl.semaphore_wait(barrier, n_dev - 1)
    for cp in local:
        cp.wait()

    def remote(i, k, src_slot, dst_slot):
        return pltpu.make_async_remote_copy(
            src_ref=bufs[i].at[src_slot], dst_ref=bufs[i].at[dst_slot],
            send_sem=send_sem.at[i, dst_slot], recv_sem=recv_sem.at[i, dst_slot],
            device_id={"ep": me ^ k}, device_id_type=MESH)

    far = remote(0, 2, 0, 2)
    near = remote(0, 1, 0, 1)
    relay = remote(0, 1, 2, 3)
    small = {k: [remote(i, k, 0, k) for i in range(1, len(bufs))] for k in range(1, n_dev)}
    for cp in small[2]:
        cp.start()
    far.start()
    for k in (3, 1):
        for cp in small[k]:
            cp.start()
    near.start()

    loads[0].wait()
    loads[1].wait()

    def silu(e, carry):
        gate_f = hg_ref[e].astype(F32)
        up_f = hu_ref[e].astype(F32)
        gate_sig = jax.nn.sigmoid(gate_f)
        gate_act = gate_f * gate_sig
        act_ref[e] = (gate_act * up_f).astype(BF16)
        fac1_ref[e] = up_f * gate_sig * (1.0 + gate_f * (1.0 - gate_sig))
        fac3_ref[e] = gate_act
        return carry

    lax.fori_loop(0, n_loc, silu, 0)

    tok = tk_ref.shape[2]
    rows = n_loc * cap

    def select(k):
        row = lax.broadcasted_iota(jnp.int32, (rows, tok), 0) + me * rows
        key = jnp.where(sl_ref[k] >= 0, tk_ref[k] * cap + sl_ref[k], -1)
        gate = gt_ref[k]
        pick = jnp.zeros((rows, tok), F32)
        gate_sel = jnp.zeros((rows, tok), F32)
        for j in range(key.shape[0]):
            hit = key[j:j + 1, :] == row
            pick = jnp.where(hit, 1.0, pick)
            gate_sel = jnp.where(hit, gate[j:j + 1, :], gate_sel)
        row1 = lax.broadcasted_iota(jnp.int32, (rows, 1), 0)
        lane = lax.broadcasted_iota(jnp.int32, ct_ref.shape[1:], 1)
        count = jnp.zeros((rows, 1), jnp.int32)
        for e in range(n_loc):
            here = jnp.sum(jnp.where(lane == me * n_loc + e, ct_ref[k], 0), axis=1, keepdims=True)
            count = jnp.where(row1 // cap == e, here, count)
        pick_ref[k] = pick.astype(BF16)
        gate_ref[k] = jnp.where(row1 % cap < count, jnp.sum(gate_sel, axis=1, keepdims=True), 0.0)

    def gated_rows(k):
        rows_k = (dot(pick_ref[k], gy_ref[k], 1, 0) * gate_ref[k]).astype(BF16)
        at = pl.multiple_of((me ^ k) * cap, cap)
        for e in range(n_loc):
            d_ref[e, pl.ds(at, cap), :] = rows_k[e * cap:(e + 1) * cap, :]

    select(0)
    gated_rows(0)
    for k in (1, 2, 3):
        for cp in small[k]:
            cp.wait()
        select(k)
    near.wait()
    gated_rows(1)
    far.wait_recv()
    relay.start()
    gated_rows(2)
    relay.wait()
    gated_rows(3)
    far.wait_send()
    for cp in loads[2:]:
        cp.wait()


def front_pass(gy, tk, sl, gt, ct, hg, hu, wd, wg, wu, x, y, n_dev, cap):
    args = (gy, tk, sl, gt, ct, hg, hu, wd, wg, wu, x, y)
    n_loc, ffn, model = wd.shape
    tok = gy.shape[0]
    rows = hg.shape[1]
    outs = [
        pltpu.VMEM((n_dev, tok, model), BF16),
        pltpu.VMEM((n_dev, n_loc * cap, tok), BF16),
        pltpu.VMEM((n_loc, rows, model), BF16),
        pltpu.VMEM((n_loc, rows, ffn), BF16),
        pltpu.VMEM((n_loc, rows, ffn), F32),
        pltpu.VMEM((n_loc, rows, ffn), F32),
        pltpu.VMEM(wd.shape, BF16),
        pltpu.VMEM((SPLIT,) + wg.shape[1:], BF16),
        pltpu.VMEM((SPLIT,) + wu.shape[1:], BF16),
        pltpu.VMEM(x.shape, BF16),
        pltpu.VMEM(y.shape, BF16),
    ]
    return pl.pallas_call(
        functools.partial(front_kernel, n_dev, cap),
        out_shape=outs,
        in_specs=[ANY] * len(args),
        out_specs=[VMEM] * len(outs),
        scratch_shapes=[
            pltpu.VMEM((n_dev,) + tk.shape, jnp.int32),
            pltpu.VMEM((n_dev,) + sl.shape, jnp.int32),
            pltpu.VMEM((n_dev,) + gt.shape, F32),
            pltpu.VMEM((n_dev,) + ct.shape, jnp.int32),
            pltpu.VMEM(hg.shape, BF16),
            pltpu.VMEM(hu.shape, BF16),
            pltpu.VMEM((n_dev, n_loc * cap, 1), F32),
            pltpu.SemaphoreType.DMA((5,)),
            pltpu.SemaphoreType.DMA((7,)),
            pltpu.SemaphoreType.DMA((5, n_dev)),
            pltpu.SemaphoreType.DMA((5, n_dev)),
        ],
        compiler_params=pltpu.CompilerParams(collective_id=0, has_side_effects=True, vmem_limit_bytes=8 * MIB),
        name="front_pass",
    )(*[pltpu.with_memory_space_constraint(a, pltpu.HBM) for a in args])


def expert_kernel(n_dev, cap, pick_ref, d_ref, act_ref, fac1_ref, fac3_ref, wd_ref, wga_ref, wua_ref, wg_in, wu_in,
                  dwd_ref, dh1_ref, dh3_ref, *rest):
    part_refs = rest[:n_dev]
    wgb_ref, wub_ref, ret_ref, stage_ref, load_sem, out_sem = rest[n_dev:]
    n_loc = wd_ref.shape[0]
    n_stage = stage_ref.shape[0]
    me = lax.axis_index("ep")
    loads = {e: (pltpu.make_async_copy(wg_in.at[e], wgb_ref.at[e - SPLIT], load_sem.at[0, e - SPLIT]),
                 pltpu.make_async_copy(wu_in.at[e], wub_ref.at[e - SPLIT], load_sem.at[1, e - SPLIT]))
             for e in range(SPLIT, n_loc)}
    for e in loads:
        for cp in loads[e]:
            cp.start()
    outs = [pltpu.make_async_copy(stage_ref.at[e % n_stage], dwd_ref.at[e], out_sem.at[e % n_stage]) for e in range(n_loc)]

    def down_grad(e):
        if e >= n_stage:
            outs[e - n_stage].wait()
        stage_ref[e % n_stage] = dot(act_ref[e], d_ref[e], 0, 0)
        outs[e].start()

    def hidden_grad(e):
        grad_h = dot(d_ref[e], wd_ref[e], 1, 1).astype(BF16).astype(F32)
        dh1_ref[e] = (grad_h * fac1_ref[e]).astype(BF16)
        dh3_ref[e] = (grad_h * fac3_ref[e]).astype(BF16)

    def row_grad(e):
        if e in loads:
            for cp in loads[e]:
                cp.wait()
        wg, wu = (wgb_ref[e - SPLIT], wub_ref[e - SPLIT]) if e in loads else (wga_ref[e], wua_ref[e])
        ret = (dot(dh1_ref[e], wg, 1, 1) + dot(dh3_ref[e], wu, 1, 1)).astype(BF16)
        for s in range(n_dev):
            ret_ref[s, e * cap:(e + 1) * cap, :] = ret[s * cap:(s + 1) * cap, :]

    down_grad(0)
    hidden_grad(0)
    for e in range(n_loc):
        if e + 1 < n_loc:
            down_grad(e + 1)
            hidden_grad(e + 1)
        row_grad(e)
    for k in range(n_dev):
        part_refs[k][...] = dot(pick_ref[k], ret_ref[me ^ k], 0, 0)
    for e in range(n_loc - n_stage, n_loc):
        outs[e].wait()


def expert_pass(pick, d, act, fac1, fac3, wd, wga, wua, wg, wu, n_dev, cap):
    n_loc, ffn, model = wd.shape
    rows = d.shape[1]
    tok = pick.shape[2]
    n_stage = 2
    late = n_loc - SPLIT
    hbm = [pltpu.with_memory_space_constraint(a, pltpu.HBM) for a in (wg, wu)]
    return pl.pallas_call(
        functools.partial(expert_kernel, n_dev, cap),
        out_shape=[
            jax.ShapeDtypeStruct((n_loc, ffn, model), F32),
            pltpu.VMEM((n_loc, rows, ffn), BF16),
            pltpu.VMEM((n_loc, rows, ffn), BF16),
        ] + [pltpu.VMEM((tok, model), F32)] * n_dev,
        in_specs=[VMEM] * 8 + [ANY] * 2,
        out_specs=[ANY, VMEM, VMEM] + [VMEM] * n_dev,
        scratch_shapes=[
            pltpu.VMEM((late,) + wg.shape[1:], BF16),
            pltpu.VMEM((late,) + wu.shape[1:], BF16),
            pltpu.VMEM((n_dev, n_loc * cap, model), BF16),
            pltpu.VMEM((n_stage, ffn, model), F32),
            pltpu.SemaphoreType.DMA((2, late)),
            pltpu.SemaphoreType.DMA((n_stage,)),
        ],
        compiler_params=pltpu.CompilerParams(vmem_limit_bytes=20 * MIB),
        cost_estimate=pl.CostEstimate(flops=10 * n_loc * rows * ffn * model, bytes_accessed=50 * MIB, transcendentals=0),
        name="expert_pass",
    )(pick, d, act, fac1, fac3, wd, wga, wua, *hbm)


def weight_kernel(x_ref, dh1_ref, dh3_ref, gy_ref, y_ref, dwg_ref, dwu_ref, gg_ref, stage, gg_acc, out_sem):
    n_loc, _, model = x_ref.shape
    top_k = y_ref.shape[1]
    half = model // 2

    def out_copy(e, s, q):
        dst = (dwg_ref, dwu_ref)[q % 2].at[e, pl.ds(half * (q // 2), half), :]
        return pltpu.make_async_copy(stage.at[s, q], dst, out_sem.at[s, q])

    def one(e, s):
        for h in range(2):
            x = x_ref[e, :, h * half:(h + 1) * half]
            for w, dh in enumerate((dh1_ref, dh3_ref)):
                q = 2 * h + w
                stage[s, q] = dot(x, dh[e], 0, 0)
                out_copy(e, s, q).start()

    def wait_all(s):
        for q in range(4):
            out_copy(0, s, q).wait()

    def body(i, carry):
        for s in range(2):
            @pl.when(i > 0)
            def _():
                wait_all(s)
            one(2 * i + s, s)

        @pl.when(i == n_loc // 2 - 2)
        def _():
            step = 8
            for b in range(y_ref.shape[0] // step):
                prod = y_ref[b * step:(b + 1) * step].astype(F32) * gy_ref[0, b * step:(b + 1) * step].astype(F32)[:, None, :]
                gg_acc[b * step:(b + 1) * step, 0:top_k] = jnp.sum(prod, axis=2)
            gg_ref[...] = gg_acc[...].T[0:top_k, :]
        return carry

    lax.fori_loop(0, n_loc // 2, body, 0)
    wait_all(0)
    wait_all(1)


def weight_pass(x, dh1, dh3, gy, y):
    n_loc, rows, model = x.shape
    ffn = dh1.shape[2]
    tok, top_k, _ = y.shape
    grad_shape = jax.ShapeDtypeStruct((n_loc, model, ffn), F32)
    return pl.pallas_call(
        weight_kernel,
        out_shape=[grad_shape, grad_shape, jax.ShapeDtypeStruct((top_k, tok), F32)],
        in_specs=[VMEM] * 5,
        out_specs=[ANY, ANY, VMEM],
        scratch_shapes=[
            pltpu.VMEM((2, 4, model // 2, ffn), F32),
            pltpu.VMEM((tok, 128), F32),
            pltpu.SemaphoreType.DMA((2, 4)),
        ],
        compiler_params=pltpu.CompilerParams(vmem_limit_bytes=20 * MIB),
        cost_estimate=pl.CostEstimate(flops=4 * n_loc * rows * ffn * model, bytes_accessed=40 * MIB, transcendentals=0),
        name="weight_pass",
    )(x, dh1, dh3, gy, y)


def solution(mesh):
    n_dev = mesh.shape["ep"]
    rows_spec = P(("dp", "ep"), None)
    cube_spec = P(("dp", "ep"), None, None)
    weight_spec = P("ep", None, None)

    def local_step(grad_y, gate_vals, topk_idx, slot_ids, pair_counts, y_routed, x_disp, h_gate, h_up, w_gate, w_up, w_down):
        cap = x_disp.shape[1] // n_dev
        gy, pick, d, act, fac1, fac3, wd, wga, wua, x, y = front_pass(
            grad_y, topk_idx.T, slot_ids.T, gate_vals.T, pair_counts, h_gate, h_up, w_down, w_gate, w_up, x_disp, y_routed, n_dev, cap)
        dwd, dh1, dh3, *parts = expert_pass(pick, d, act, fac1, fac3, wd, wga, wua, w_gate, w_up, n_dev, cap)
        back = [lax.ppermute(parts[k], "ep", [(i, i ^ k) for i in range(n_dev)]) for k in range(1, n_dev)]
        dwg, dwu, gg = weight_pass(x, dh1, dh3, gy, y)
        total = parts[0]
        for b in back:
            total = total + b
        return total.astype(BF16), gg.T, dwg, dwu, dwd

    return jax.shard_map(local_step, mesh=mesh, in_specs=(rows_spec, rows_spec, rows_spec, rows_spec, rows_spec, cube_spec, cube_spec, cube_spec, cube_spec, weight_spec, weight_spec, weight_spec), out_specs=(rows_spec, rows_spec, cube_spec, cube_spec, cube_spec), check_vma=False)
```

time: 44.4 us -> 37.7 us (0.85)
  Pallas kernels: 39.2 us -> 34.3 us
  starting transfers between devices: 3.37 us -> 1.9 us
    pallas_call x1, Pallas kernels: 17.1 us -> 12.2 us  [expert_pass(): pl.pallas_call(functools.partial(expert_kernel, n_dev, cap), out_shape=[j...]
    ppermute x3, starting transfers between devices: 3.37 us -> 1.9 us  [local_step(): lax.ppermute(parts[k], 'ep', [(i, i ^ k) for i in range(n_dev)])]
  transfers between devices with their start and end apart: 3 -> 3, of which waited for: 1 -> 0; matrix products, arithmetic and copies ran while one was open for 0% -> 0% of each run, Pallas kernels for 27% -> 31%
where the time goes in v3:
time: 37.7 us; the launch traced here: 37.6 us
  Pallas kernels  34.3 us (91%)
  starting transfers between devices  1.9 us (5%)
  other arithmetic  0.72 us (2%)
  between operations  0.68 us (2%)
    pallas_call x1, Pallas kernels, expert_pass(): pl.pallas_call(functools.partial(expert_kernel, n_dev, cap), out_shape=[j...  12.2 us
    pallas_call x1, Pallas kernels, weight_pass(): pl.pallas_call(weight_kernel, out_shape=[grad_shape, grad_shape, jax.Shap...  11.8 us
    pallas_call x1, Pallas kernels, front_pass(): pl.pallas_call(functools.partial(front_kernel, n_dev, cap), out_shape=out...  10.3 us
    ppermute x3, starting transfers between devices, local_step(): lax.ppermute(parts[k], 'ep', [(i, i ^ k) for i in range(n_dev)])  1.9 us
  transfers between devices with their start and end apart: 3, of which 0 were waited for; matrix products, arithmetic and copies ran while one was open for 0% of the time, Pallas kernels for 31%

profile of v3, /device:TPU:0, one launch (start us, length us, event | category | flops | bytes accessed | tf_op | source)
XLA Modules:
  0.0 37.6 jit_solution(5843741587984926659)
XLA Ops:
  0.6 10.3 %front_pass.1 = (bf16[4,64,1024]{2,1,0:T(8,128)(2,1)S(1)}, bf16[4,256,64]{2,1,0:T(8,128)(2,1)S(1)}, bf16[8,128,1024]{2,1,0:T(8,128)(2,1)S(1)}, bf16[8,128,512]{2...) custom-call(bf16[64,1024]{1,0:T(8,128)(2,1)} %gy_in.1, ...), custom_call_target="tpu_custom_call" | custom-call | tf_op jit(solution)/shard_map/front_pass/pallas_call | solution.py:142
  10.9 12.2 %expert_pass.1 = (f32[8,512,1024]{2,1,0:T(8,128)}, bf16[8,128,512]{2,1,0:T(8,128)(2,1)S(1)}, bf16[8,128,512]{2,1,0:T(8,128)(2,1)S(1)}, f32[64,1024]{1,0:T(8,128)...) custom-call(bf16[4,256,64]{2,1,0:T(8,128)(2,1)S(1)} %get-tuple-element.26.pick_ref, ...), custom_call_target="tpu_custom_call" | custom-call | flops 5368709120 | bytes 52428800 | tf_op jit(solution)/shard_map/expert_pass/pallas_call | solution.py:220
  23.1 0.2 collective-permute-start
  23.3 1.4 %collective-permute-start.1 = (f32[64,1024]{1,0:T(8,128)S(1)}, f32[64,1024]{1,0:T(8,128)S(1)}, u32[]{:S(2)}, u32[]{:S(2)}) collective-permute-start(f32[64,1024]{1,0:T(8,128)S(1)} %get-tuple-element.36), channel_id=1, source_target_pairs={{0,2},{1,3},{2,0},{3,1},{4,6},{5,7},{6,4},{7,5},{8,10},{9,11},{10,... | collective-permute-start | bytes 786440 | tf_op jit(solution)/shard_map/ppermute | solution.py:317
  24.7 0.3 collective-permute-start.2
  25.0 11.8 %weight_pass.1 = (f32[8,1024,512]{2,1,0:T(8,128)}, f32[8,1024,512]{2,1,0:T(8,128)}, f32[8,64]{1,0:T(8,128)}) custom-call(bf16[8,128,1024]{2,1,0:T(8,128)(2,1)S(1)} %get-tuple-element.38.x_ref, bf16[8,128,512]{2,1,0:T(8,128)(2,1)S(1)} %get-tuple-element.39.dh1_ref, bf16[8,128,512]{2,1,0:T(8,128)(2,1)S(1)} %get-tuple-element.40.dh3_ref, ...), custom_call_target="tpu_custom_call" | custom-call | flops 2147483648 | bytes 41943040 | tf_op jit(solution)/shard_map/weight_pass/pallas_call | solution.py:290
  36.8 0.0 collective-permute-done
  36.9 0.0 collective-permute-done.1
  36.9 0.0 collective-permute-done.2
  36.9 0.7 %add_convert_fusion = bf16[64,1024]{1,0:T(8,128)(2,1)} fusion(f32[64,1024]{1,0:T(8,128)S(1)} %collective-permute-done.2, f32[64,1024]{1,0:T(8,128)S(1)} %collective-permute-done.1, f32[64,1024]{1,0:T(8,128)S(1)} %get-tuple-element.34, f32[64,1024]{1,0:T(8,128)S(1)} %collective-permute-done), kind=kLoop, calls=%fused_computation | loop fusion | flops 262144 | bytes 1179648 | tf_op jit(solution)/shard_map/convert_element_type | solution.py:322
Async XLA Ops:
  23.1 13.7 %collective-permute-start = (f32[64,1024]{1,0:T(8,128)S(1)}, f32[64,1024]{1,0:T(8,128)S(1)}, u32[]{:S(2)}, u32[]{:S(2)}) collective-permute-start(f32[64,1024]{1,0:T(8,128)S(1)} %get-tuple-element.35), channel_id=1, source_target_pairs={{0,1},{1,0},{2,3},{3,2},{4,5},{5,4},{6,7},{7,6},{8,9},{9,8},{10,11... | collective-permute-start | bytes 786440 | tf_op jit(solution)/shard_map/ppermute | solution.py:317
  23.3 13.6 %collective-permute-start.1 = (f32[64,1024]{1,0:T(8,128)S(1)}, f32[64,1024]{1,0:T(8,128)S(1)}, u32[]{:S(2)}, u32[]{:S(2)}) collective-permute-start(f32[64,1024]{1,0:T(8,128)S(1)} %get-tuple-element.36), channel_id=1, source_target_pairs={{0,2},{1,3},{2,0},{3,1},{4,6},{5,7},{6,4},{7,5},{8,10},{9,11},{10,... | collective-permute-start | bytes 786440 | tf_op jit(solution)/shard_map/ppermute | solution.py:317
  24.7 12.2 %collective-permute-start.2 = (f32[64,1024]{1,0:T(8,128)S(1)}, f32[64,1024]{1,0:T(8,128)S(1)}, u32[]{:S(2)}, u32[]{:S(2)}) collective-permute-start(f32[64,1024]{1,0:T(8,128)S(1)} %get-tuple-element.37), channel_id=1, source_target_pairs={{0,3},{1,2},{2,1},{3,0},{4,7},{5,6},{6,5},{7,4},{8,11},{9,10},{10,... | collective-permute-start | bytes 786440 | tf_op jit(solution)/shard_map/ppermute | solution.py:317

commit v4 on v3

--- a/solution.py
+++ b/solution.py
@@ -13,7 +13,7 @@
 ANY = pl.BlockSpec(memory_space=pl.ANY)
 VMEM = pl.BlockSpec(memory_space=pltpu.VMEM)
 MIB = 2**20
-SPLIT = 4
+SPLIT = 5
 
 
 def dot(a, b, ca, cb):
@@ -165,9 +165,10 @@
 def expert_kernel(n_dev, cap, pick_ref, d_ref, act_ref, fac1_ref, fac3_ref, wd_ref, wga_ref, wua_ref, wg_in, wu_in,
                   dwd_ref, dh1_ref, dh3_ref, *rest):
     part_refs = rest[:n_dev]
-    wgb_ref, wub_ref, ret_ref, stage_ref, load_sem, out_sem = rest[n_dev:]
+    wgb_ref, wub_ref, ret_ref, stage_ref, wdt_ref, wgt_ref, wut_ref, load_sem, out_sem = rest[n_dev:]
     n_loc = wd_ref.shape[0]
     n_stage = stage_ref.shape[0]
+    n_turn = wut_ref.shape[2]
     me = lax.axis_index("ep")
     loads = {e: (pltpu.make_async_copy(wg_in.at[e], wgb_ref.at[e - SPLIT], load_sem.at[0, e - SPLIT]),
                  pltpu.make_async_copy(wu_in.at[e], wub_ref.at[e - SPLIT], load_sem.at[1, e - SPLIT]))
@@ -177,6 +178,20 @@
             cp.start()
     outs = [pltpu.make_async_copy(stage_ref.at[e % n_stage], dwd_ref.at[e], out_sem.at[e % n_stage]) for e in range(n_loc)]
 
+    def weights(e):
+        return (wgb_ref[e - SPLIT], wub_ref[e - SPLIT]) if e in loads else (wga_ref[e], wua_ref[e])
+
+    def turn_down(e):
+        wdt_ref[e % 2] = wd_ref[e].T
+
+    def turn_gate_up(e):
+        if e in loads:
+            for cp in loads[e]:
+                cp.wait()
+        wg, wu = weights(e)
+        wgt_ref[e % 2] = wg.T
+        wut_ref[e % 2] = wu[:n_turn].T
+
     def down_grad(e):
         if e >= n_stage:
             outs[e - n_stage].wait()
@@ -184,25 +199,32 @@
         outs[e].start()
 
     def hidden_grad(e):
-        grad_h = dot(d_ref[e], wd_ref[e], 1, 1).astype(BF16).astype(F32)
+        grad_h = dot(d_ref[e], wd_ref[e], 1, 1) if e == 0 else dot(d_ref[e], wdt_ref[e % 2], 1, 0)
+        grad_h = grad_h.astype(BF16).astype(F32)
         dh1_ref[e] = (grad_h * fac1_ref[e]).astype(BF16)
         dh3_ref[e] = (grad_h * fac3_ref[e]).astype(BF16)
 
     def row_grad(e):
-        if e in loads:
-            for cp in loads[e]:
-                cp.wait()
-        wg, wu = (wgb_ref[e - SPLIT], wub_ref[e - SPLIT]) if e in loads else (wga_ref[e], wua_ref[e])
-        ret = (dot(dh1_ref[e], wg, 1, 1) + dot(dh3_ref[e], wu, 1, 1)).astype(BF16)
+        wg, wu = weights(e)
+        if e == 0:
+            ret = dot(dh1_ref[e], wg, 1, 1) + dot(dh3_ref[e], wu, 1, 1)
+        else:
+            up = [dot(dh3_ref[e], wut_ref[e % 2], 1, 0), dot(dh3_ref[e], wu[n_turn:], 1, 1)]
+            ret = dot(dh1_ref[e], wgt_ref[e % 2], 1, 0) + jnp.concatenate(up, axis=1)
+        ret = ret.astype(BF16)
         for s in range(n_dev):
             ret_ref[s, e * cap:(e + 1) * cap, :] = ret[s * cap:(s + 1) * cap, :]
 
     down_grad(0)
     hidden_grad(0)
+    turn_down(1)
     for e in range(n_loc):
         if e + 1 < n_loc:
             down_grad(e + 1)
             hidden_grad(e + 1)
+            turn_gate_up(e + 1)
+        if e + 2 < n_loc:
+            turn_down(e + 2)
         row_grad(e)
     for k in range(n_dev):
         part_refs[k][...] = dot(pick_ref[k], ret_ref[me ^ k], 0, 0)
@@ -231,19 +253,23 @@
             pltpu.VMEM((late,) + wu.shape[1:], BF16),
             pltpu.VMEM((n_dev, n_loc * cap, model), BF16),
             pltpu.VMEM((n_stage, ffn, model), F32),
+            pltpu.VMEM((2, model, ffn), BF16),
+            pltpu.VMEM((2, ffn, model), BF16),
+            pltpu.VMEM((2, ffn, model // 2), BF16),
             pltpu.SemaphoreType.DMA((2, late)),
             pltpu.SemaphoreType.DMA((n_stage,)),
         ],
-        compiler_params=pltpu.CompilerParams(vmem_limit_bytes=20 * MIB),
+        compiler_params=pltpu.CompilerParams(vmem_limit_bytes=(15 + 2 * late) * MIB + MIB // 2),
         cost_estimate=pl.CostEstimate(flops=10 * n_loc * rows * ffn * model, bytes_accessed=50 * MIB, transcendentals=0),
         name="expert_pass",
     )(pick, d, act, fac1, fac3, wd, wga, wua, *hbm)
 
 
-def weight_kernel(x_ref, dh1_ref, dh3_ref, gy_ref, y_ref, dwg_ref, dwu_ref, gg_ref, stage, gg_acc, out_sem):
+def weight_kernel(x_ref, dh1_ref, dh3_ref, gy_ref, y_ref, dwg_ref, dwu_ref, gg_ref, stage, gg_acc, gg_out, out_sem, gg_sem):
     n_loc, _, model = x_ref.shape
     top_k = y_ref.shape[1]
     half = model // 2
+    gg_copy = pltpu.make_async_copy(gg_out, gg_ref, gg_sem)
 
     def out_copy(e, s, q):
         dst = (dwg_ref, dwu_ref)[q % 2].at[e, pl.ds(half * (q // 2), half), :]
@@ -274,10 +300,12 @@
             for b in range(y_ref.shape[0] // step):
                 prod = y_ref[b * step:(b + 1) * step].astype(F32) * gy_ref[0, b * step:(b + 1) * step].astype(F32)[:, None, :]
                 gg_acc[b * step:(b + 1) * step, 0:top_k] = jnp.sum(prod, axis=2)
-            gg_ref[...] = gg_acc[...].T[0:top_k, :]
+            gg_out[...] = gg_acc[...].T[0:top_k, :]
+            gg_copy.start()
         return carry
 
     lax.fori_loop(0, n_loc // 2, body, 0)
+    gg_copy.wait()
     wait_all(0)
     wait_all(1)
 
@@ -291,11 +319,13 @@
         weight_kernel,
         out_shape=[grad_shape, grad_shape, jax.ShapeDtypeStruct((top_k, tok), F32)],
         in_specs=[VMEM] * 5,
-        out_specs=[ANY, ANY, VMEM],
+        out_specs=[ANY, ANY, ANY],
         scratch_shapes=[
             pltpu.VMEM((2, 4, model // 2, ffn), F32),
             pltpu.VMEM((tok, 128), F32),
+            pltpu.VMEM((top_k, tok), F32),
             pltpu.SemaphoreType.DMA((2, 4)),
+            pltpu.SemaphoreType.DMA,
         ],
         compiler_params=pltpu.CompilerParams(vmem_limit_bytes=20 * MIB),
         cost_estimate=pl.CostEstimate(flops=4 * n_loc * rows * ffn * model, bytes_accessed=40 * MIB, transcendentals=0),

time: 37.7 us -> 35.3 us (0.936)
  Pallas kernels: 34.3 us -> 31.3 us
  waiting for transfers between devices: 0.01 us -> 0.6 us
    pallas_call x1, Pallas kernels: 12.2 us -> 9.76 us  [expert_pass(): pl.pallas_call(functools.partial(expert_kernel, n_dev, cap), out_shape=[j...]
    ppermute x3, waiting for transfers between devices: 0.01 us -> 0.6 us  [local_step(): lax.ppermute(parts[k], 'ep', [(i, i ^ k) for i in range(n_dev)])]
    pallas_call x1, Pallas kernels: 11.8 us -> 11.3 us  [weight_pass(): pl.pallas_call(weight_kernel, out_shape=[grad_shape, grad_shape, jax.Shap...]
  transfers between devices with their start and end apart: 3 -> 3, of which waited for: 0 -> 1; matrix products, arithmetic and copies ran while one was open for 0% -> 0% of each run, Pallas kernels for 31% -> 32%
where the time goes in v4:
time: 35.3 us; the launch traced here: 35.2 us
  Pallas kernels  31.3 us (89%)
  starting transfers between devices  1.9 us (5%)
  other arithmetic  0.71 us (2%)
  between operations  0.68 us (2%)
  waiting for transfers between devices  0.6 us (2%)
    pallas_call x1, Pallas kernels, weight_pass(): pl.pallas_call(weight_kernel, out_shape=[grad_shape, grad_shape, jax.Shap...  11.3 us
    pallas_call x1, Pallas kernels, front_pass(): pl.pallas_call(functools.partial(front_kernel, n_dev, cap), out_shape=out...  10.3 us
    pallas_call x1, Pallas kernels, expert_pass(): pl.pallas_call(functools.partial(expert_kernel, n_dev, cap), out_shape=[j...  9.76 us
    ppermute x3, starting transfers between devices, local_step(): lax.ppermute(parts[k], 'ep', [(i, i ^ k) for i in range(n_dev)])  1.9 us
    convert_element_type x1, other arithmetic, local_step(): return (total.astype(BF16), gg.T, dwg, dwu, dwd)  0.71 us
  transfers between devices with their start and end apart: 3, of which 1 were waited for; matrix products, arithmetic and copies ran while one was open for 0% of the time, Pallas kernels for 32%

profile of v4, /device:TPU:0, one launch (start us, length us, event | category | flops | bytes accessed | tf_op | source)
XLA Modules:
  0.0 35.2 jit_solution(416088513233211647)
XLA Ops:
  0.6 10.3 %front_pass.1 = (bf16[4,64,1024]{2,1,0:T(8,128)(2,1)S(1)}, bf16[4,256,64]{2,1,0:T(8,128)(2,1)S(1)}, bf16[8,128,1024]{2,1,0:T(8,128)(2,1)S(1)}, bf16[8,128,512]{2...) custom-call(bf16[64,1024]{1,0:T(8,128)(2,1)} %gy_in.1, ...), custom_call_target="tpu_custom_call" | custom-call | tf_op jit(solution)/shard_map/front_pass/pallas_call | solution.py:142
  10.9 9.8 %expert_pass.1 = (f32[8,512,1024]{2,1,0:T(8,128)}, bf16[8,128,512]{2,1,0:T(8,128)(2,1)S(1)}, bf16[8,128,512]{2,1,0:T(8,128)(2,1)S(1)}, f32[64,1024]{1,0:T(8,128)...) custom-call(bf16[4,256,64]{2,1,0:T(8,128)(2,1)S(1)} %get-tuple-element.26.pick_ref, ...), custom_call_target="tpu_custom_call" | custom-call | flops 5368709120 | bytes 52428800 | tf_op jit(solution)/shard_map/expert_pass/pallas_call | solution.py:242
  20.7 0.2 collective-permute-start
  20.9 1.4 %collective-permute-start.1 = (f32[64,1024]{1,0:T(8,128)S(1)}, f32[64,1024]{1,0:T(8,128)S(1)}, u32[]{:S(2)}, u32[]{:S(2)}) collective-permute-start(f32[64,1024]{1,0:T(8,128)S(1)} %get-tuple-element.36), channel_id=1, source_target_pairs={{0,2},{1,3},{2,0},{3,1},{4,6},{5,7},{6,4},{7,5},{8,10},{9,11},{10,... | collective-permute-start | bytes 786440 | tf_op jit(solution)/shard_map/ppermute | solution.py:347
  22.3 0.3 collective-permute-start.2
  22.6 11.3 %weight_pass.1 = (f32[8,1024,512]{2,1,0:T(8,128)}, f32[8,1024,512]{2,1,0:T(8,128)}, f32[8,64]{1,0:T(8,128)}) custom-call(bf16[8,128,1024]{2,1,0:T(8,128)(2,1)S(1)} %get-tuple-element.38.x_ref, bf16[8,128,512]{2,1,0:T(8,128)(2,1)S(1)} %get-tuple-element.39.dh1_ref, bf16[8,128,512]{2,1,0:T(8,128)(2,1)S(1)} %get-tuple-element.40.dh3_ref, ...), custom_call_target="tpu_custom_call" | custom-call | flops 2147483648 | bytes 41943040 | tf_op jit(solution)/shard_map/weight_pass/pallas_call | solution.py:318
  33.8 0.0 collective-permute-done
  33.9 0.0 collective-permute-done.1
  33.9 0.6 %collective-permute-done.2 = f32[64,1024]{1,0:T(8,128)S(1)} collective-permute-done((f32[64,1024]{1,0:T(8,128)S(1)}, f32[64,1024]{1,0:T(8,128)S(1)}, u32[]{:S(2)}, u32[]{:S(2)}) %collective-permute-start.2) | collective-permute-done | bytes 262176 | tf_op jit(solution)/shard_map/ppermute | solution.py:347
  34.5 0.7 %add_convert_fusion = bf16[64,1024]{1,0:T(8,128)(2,1)} fusion(f32[64,1024]{1,0:T(8,128)S(1)} %collective-permute-done.2, f32[64,1024]{1,0:T(8,128)S(1)} %collective-permute-done.1, f32[64,1024]{1,0:T(8,128)S(1)} %get-tuple-element.34, f32[64,1024]{1,0:T(8,128)S(1)} %collective-permute-done), kind=kLoop, calls=%fused_computation | loop fusion | flops 262144 | bytes 1179648 | tf_op jit(solution)/shard_map/convert_element_type | solution.py:352
Async XLA Ops:
  20.7 13.2 %collective-permute-start = (f32[64,1024]{1,0:T(8,128)S(1)}, f32[64,1024]{1,0:T(8,128)S(1)}, u32[]{:S(2)}, u32[]{:S(2)}) collective-permute-start(f32[64,1024]{1,0:T(8,128)S(1)} %get-tuple-element.35), channel_id=1, source_target_pairs={{0,1},{1,0},{2,3},{3,2},{4,5},{5,4},{6,7},{7,6},{8,9},{9,8},{10,11... | collective-permute-start | bytes 786440 | tf_op jit(solution)/shard_map/ppermute | solution.py:347
  20.9 13.0 %collective-permute-start.1 = (f32[64,1024]{1,0:T(8,128)S(1)}, f32[64,1024]{1,0:T(8,128)S(1)}, u32[]{:S(2)}, u32[]{:S(2)}) collective-permute-start(f32[64,1024]{1,0:T(8,128)S(1)} %get-tuple-element.36), channel_id=1, source_target_pairs={{0,2},{1,3},{2,0},{3,1},{4,6},{5,7},{6,4},{7,5},{8,10},{9,11},{10,... | collective-permute-start | bytes 786440 | tf_op jit(solution)/shard_map/ppermute | solution.py:347
  22.3 12.2 %collective-permute-start.2 = (f32[64,1024]{1,0:T(8,128)S(1)}, f32[64,1024]{1,0:T(8,128)S(1)}, u32[]{:S(2)}, u32[]{:S(2)}) collective-permute-start(f32[64,1024]{1,0:T(8,128)S(1)} %get-tuple-element.37), channel_id=1, source_target_pairs={{0,3},{1,2},{2,1},{3,0},{4,7},{5,6},{6,5},{7,4},{8,11},{9,10},{10,... | collective-permute-start | bytes 786440 | tf_op jit(solution)/shard_map/ppermute | solution.py:347

commit v5 on v4

--- a/solution.py
+++ b/solution.py
@@ -13,15 +13,16 @@
 ANY = pl.BlockSpec(memory_space=pl.ANY)
 VMEM = pl.BlockSpec(memory_space=pltpu.VMEM)
 MIB = 2**20
-SPLIT = 5
+SPLIT = 6
+AHEAD = 3
 
 
 def dot(a, b, ca, cb):
     return lax.dot_general(a, b, (((ca,), (cb,)), ((), ())), preferred_element_type=F32)
 
 
-def front_kernel(n_dev, cap, gy_in, tk_in, sl_in, gt_in, ct_in, hg_in, hu_in, wd_in, wg_in, wu_in, x_in, y_in,
-                 gy_ref, pick_ref, d_ref, act_ref, fac1_ref, fac3_ref, wd_ref, wg_ref, wu_ref, x_ref, y_ref,
+def front_kernel(n_dev, cap, gy_in, tk_in, sl_in, gt_in, ct_in, hg_in, hu_in, wd_in, wg_in, wu_in, x_in,
+                 gy_ref, pick_ref, d_ref, act_ref, fac1_ref, fac3_ref, wd_ref, wg_ref, wu_ref, x_ref,
                  tk_ref, sl_ref, gt_ref, ct_ref, hg_ref, hu_ref, gate_ref, local_sem, load_sem, send_sem, recv_sem):
     me = lax.axis_index("ep")
     n_loc = d_ref.shape[0]
@@ -29,7 +30,7 @@
     local = [pltpu.make_async_copy(a, b.at[0], local_sem.at[i])
              for i, (a, b) in enumerate(zip((gy_in, tk_in, sl_in, gt_in, ct_in), bufs))]
     pairs = [(hg_in, hg_ref), (hu_in, hu_ref), (wd_in, wd_ref), (wg_in.at[pl.ds(0, SPLIT)], wg_ref),
-             (wu_in.at[pl.ds(0, SPLIT)], wu_ref), (x_in, x_ref), (y_in, y_ref)]
+             (wu_in.at[pl.ds(0, SPLIT)], wu_ref), (x_in, x_ref)]
     loads = [pltpu.make_async_copy(a, b, load_sem.at[i]) for i, (a, b) in enumerate(pairs)]
     for cp in local:
         cp.start()
@@ -68,7 +69,7 @@
         up_f = hu_ref[e].astype(F32)
         gate_sig = jax.nn.sigmoid(gate_f)
         gate_act = gate_f * gate_sig
-        act_ref[e] = (gate_act * up_f).astype(BF16)
+        act_ref[e] = (gate_act * up_f).astype(BF16).T
         fac1_ref[e] = up_f * gate_sig * (1.0 + gate_f * (1.0 - gate_sig))
         fac3_ref[e] = gate_act
         return carry
@@ -121,8 +122,8 @@
         cp.wait()
 
 
-def front_pass(gy, tk, sl, gt, ct, hg, hu, wd, wg, wu, x, y, n_dev, cap):
-    args = (gy, tk, sl, gt, ct, hg, hu, wd, wg, wu, x, y)
+def front_pass(gy, tk, sl, gt, ct, hg, hu, wd, wg, wu, x, n_dev, cap):
+    args = (gy, tk, sl, gt, ct, hg, hu, wd, wg, wu, x)
     n_loc, ffn, model = wd.shape
     tok = gy.shape[0]
     rows = hg.shape[1]
@@ -130,14 +131,13 @@
         pltpu.VMEM((n_dev, tok, model), BF16),
         pltpu.VMEM((n_dev, n_loc * cap, tok), BF16),
         pltpu.VMEM((n_loc, rows, model), BF16),
-        pltpu.VMEM((n_loc, rows, ffn), BF16),
+        pltpu.VMEM((n_loc, ffn, rows), BF16),
         pltpu.VMEM((n_loc, rows, ffn), F32),
         pltpu.VMEM((n_loc, rows, ffn), F32),
         pltpu.VMEM(wd.shape, BF16),
         pltpu.VMEM((SPLIT,) + wg.shape[1:], BF16),
         pltpu.VMEM((SPLIT,) + wu.shape[1:], BF16),
         pltpu.VMEM(x.shape, BF16),
-        pltpu.VMEM(y.shape, BF16),
     ]
     return pl.pallas_call(
         functools.partial(front_kernel, n_dev, cap),
@@ -153,11 +153,11 @@
             pltpu.VMEM(hu.shape, BF16),
             pltpu.VMEM((n_dev, n_loc * cap, 1), F32),
             pltpu.SemaphoreType.DMA((5,)),
-            pltpu.SemaphoreType.DMA((7,)),
+            pltpu.SemaphoreType.DMA((6,)),
             pltpu.SemaphoreType.DMA((5, n_dev)),
             pltpu.SemaphoreType.DMA((5, n_dev)),
         ],
-        compiler_params=pltpu.CompilerParams(collective_id=0, has_side_effects=True, vmem_limit_bytes=8 * MIB),
+        compiler_params=pltpu.CompilerParams(collective_id=0, has_side_effects=True, vmem_limit_bytes=5 * MIB),
         name="front_pass",
     )(*[pltpu.with_memory_space_constraint(a, pltpu.HBM) for a in args])
 
@@ -173,9 +173,6 @@
     loads = {e: (pltpu.make_async_copy(wg_in.at[e], wgb_ref.at[e - SPLIT], load_sem.at[0, e - SPLIT]),
                  pltpu.make_async_copy(wu_in.at[e], wub_ref.at[e - SPLIT], load_sem.at[1, e - SPLIT]))
              for e in range(SPLIT, n_loc)}
-    for e in loads:
-        for cp in loads[e]:
-            cp.start()
     outs = [pltpu.make_async_copy(stage_ref.at[e % n_stage], dwd_ref.at[e], out_sem.at[e % n_stage]) for e in range(n_loc)]
 
     def weights(e):
@@ -195,7 +192,7 @@
     def down_grad(e):
         if e >= n_stage:
             outs[e - n_stage].wait()
-        stage_ref[e % n_stage] = dot(act_ref[e], d_ref[e], 0, 0)
+        stage_ref[e % n_stage] = dot(act_ref[e], d_ref[e], 1, 0)
         outs[e].start()
 
     def hidden_grad(e):
@@ -219,6 +216,9 @@
     hidden_grad(0)
     turn_down(1)
     for e in range(n_loc):
+        if e + AHEAD in loads:
+            for cp in loads[e + AHEAD]:
+                cp.start()
         if e + 1 < n_loc:
             down_grad(e + 1)
             hidden_grad(e + 1)
@@ -236,7 +236,7 @@
     n_loc, ffn, model = wd.shape
     rows = d.shape[1]
     tok = pick.shape[2]
-    n_stage = 2
+    n_stage = 4
     late = n_loc - SPLIT
     hbm = [pltpu.with_memory_space_constraint(a, pltpu.HBM) for a in (wg, wu)]
     return pl.pallas_call(
@@ -259,17 +259,19 @@
             pltpu.SemaphoreType.DMA((2, late)),
             pltpu.SemaphoreType.DMA((n_stage,)),
         ],
-        compiler_params=pltpu.CompilerParams(vmem_limit_bytes=(15 + 2 * late) * MIB + MIB // 2),
+        compiler_params=pltpu.CompilerParams(vmem_limit_bytes=(16 + 2 * late) * MIB),
         cost_estimate=pl.CostEstimate(flops=10 * n_loc * rows * ffn * model, bytes_accessed=50 * MIB, transcendentals=0),
         name="expert_pass",
     )(pick, d, act, fac1, fac3, wd, wga, wua, *hbm)
 
 
-def weight_kernel(x_ref, dh1_ref, dh3_ref, gy_ref, y_ref, dwg_ref, dwu_ref, gg_ref, stage, gg_acc, gg_out, out_sem, gg_sem):
+def weight_kernel(x_ref, dh1_ref, dh3_ref, gy_ref, y_in, dwg_ref, dwu_ref, gg_ref, y_ref, stage, gg_acc, gg_out, out_sem, gg_sem):
     n_loc, _, model = x_ref.shape
     top_k = y_ref.shape[1]
     half = model // 2
-    gg_copy = pltpu.make_async_copy(gg_out, gg_ref, gg_sem)
+    gg_copy = pltpu.make_async_copy(gg_out, gg_ref, gg_sem.at[0])
+    y_copy = pltpu.make_async_copy(y_in, y_ref, gg_sem.at[1])
+    y_copy.start()
 
     def out_copy(e, s, q):
         dst = (dwg_ref, dwu_ref)[q % 2].at[e, pl.ds(half * (q // 2), half), :]
@@ -296,6 +298,7 @@
 
         @pl.when(i == n_loc // 2 - 2)
         def _():
+            y_copy.wait()
             step = 8
             for b in range(y_ref.shape[0] // step):
                 prod = y_ref[b * step:(b + 1) * step].astype(F32) * gy_ref[0, b * step:(b + 1) * step].astype(F32)[:, None, :]
@@ -318,19 +321,20 @@
     return pl.pallas_call(
         weight_kernel,
         out_shape=[grad_shape, grad_shape, jax.ShapeDtypeStruct((top_k, tok), F32)],
-        in_specs=[VMEM] * 5,
+        in_specs=[VMEM] * 4 + [ANY],
         out_specs=[ANY, ANY, ANY],
         scratch_shapes=[
+            pltpu.VMEM(y.shape, BF16),
             pltpu.VMEM((2, 4, model // 2, ffn), F32),
             pltpu.VMEM((tok, 128), F32),
             pltpu.VMEM((top_k, tok), F32),
             pltpu.SemaphoreType.DMA((2, 4)),
-            pltpu.SemaphoreType.DMA,
+            pltpu.SemaphoreType.DMA((2,)),
         ],
         compiler_params=pltpu.CompilerParams(vmem_limit_bytes=20 * MIB),
         cost_estimate=pl.CostEstimate(flops=4 * n_loc * rows * ffn * model, bytes_accessed=40 * MIB, transcendentals=0),
         name="weight_pass",
-    )(x, dh1, dh3, gy, y)
+    )(x, dh1, dh3, gy, pltpu.with_memory_space_constraint(y, pltpu.HBM))
 
 
 def solution(mesh):
@@ -341,11 +345,11 @@
 
     def local_step(grad_y, gate_vals, topk_idx, slot_ids, pair_counts, y_routed, x_disp, h_gate, h_up, w_gate, w_up, w_down):
         cap = x_disp.shape[1] // n_dev
-        gy, pick, d, act, fac1, fac3, wd, wga, wua, x, y = front_pass(
-            grad_y, topk_idx.T, slot_ids.T, gate_vals.T, pair_counts, h_gate, h_up, w_down, w_gate, w_up, x_disp, y_routed, n_dev, cap)
+        gy, pick, d, act, fac1, fac3, wd, wga, wua, x = front_pass(
+            grad_y, topk_idx.T, slot_ids.T, gate_vals.T, pair_counts, h_gate, h_up, w_down, w_gate, w_up, x_disp, n_dev, cap)
         dwd, dh1, dh3, *parts = expert_pass(pick, d, act, fac1, fac3, wd, wga, wua, w_gate, w_up, n_dev, cap)
         back = [lax.ppermute(parts[k], "ep", [(i, i ^ k) for i in range(n_dev)]) for k in range(1, n_dev)]
-        dwg, dwu, gg = weight_pass(x, dh1, dh3, gy, y)
+        dwg, dwu, gg = weight_pass(x, dh1, dh3, gy, y_routed)
         total = parts[0]
         for b in back:
             total = total + b

time: 35.3 us -> 34.3 us (0.972)
  Pallas kernels: 31.3 us -> 30.3 us
    pallas_call x1, Pallas kernels: 9.76 us -> 8.83 us  [expert_pass(): pl.pallas_call(functools.partial(expert_kernel, n_dev, cap), out_shape=[j...]
  transfers between devices with their start and end apart: 3 -> 3, of which waited for: 1 -> 1; matrix products, arithmetic and copies ran while one was open for 0% -> 0% of each run, Pallas kernels for 32% -> 33%
where the time goes in v5:
time: 34.3 us; the launch traced here: 34.2 us
  Pallas kernels  30.3 us (88%)
  starting transfers between devices  1.9 us (6%)
  other arithmetic  0.71 us (2%)
  between operations  0.68 us (2%)
  waiting for transfers between devices  0.6 us (2%)
    pallas_call x1, Pallas kernels, weight_pass(): pl.pallas_call(weight_kernel, out_shape=[grad_shape, grad_shape, jax.Shap...  11.3 us
    pallas_call x1, Pallas kernels, front_pass(): pl.pallas_call(functools.partial(front_kernel, n_dev, cap), out_shape=out...  10.2 us
    pallas_call x1, Pallas kernels, expert_pass(): pl.pallas_call(functools.partial(expert_kernel, n_dev, cap), out_shape=[j...  8.83 us
    ppermute x3, starting transfers between devices, local_step(): lax.ppermute(parts[k], 'ep', [(i, i ^ k) for i in range(n_dev)])  1.9 us
    convert_element_type x1, other arithmetic, local_step(): return (total.astype(BF16), gg.T, dwg, dwu, dwd)  0.71 us
  transfers between devices with their start and end apart: 3, of which 1 were waited for; matrix products, arithmetic and copies ran while one was open for 0% of the time, Pallas kernels for 33%

profile of v5, /device:TPU:0, one launch (start us, length us, event | category | flops | bytes accessed | tf_op | source)
XLA Modules:
  0.0 34.2 jit_solution(10033550452149504241)
XLA Ops:
  0.6 10.2 %front_pass.1 = (bf16[4,64,1024]{2,1,0:T(8,128)(2,1)S(1)}, bf16[4,256,64]{2,1,0:T(8,128)(2,1)S(1)}, bf16[8,128,1024]{2,1,0:T(8,128)(2,1)S(1)}, bf16[8,512,128]{2...) custom-call(bf16[64,1024]{1,0:T(8,128)(2,1)} %gy_in.1, ...), custom_call_target="tpu_custom_call" | custom-call | tf_op jit(solution)/shard_map/front_pass/pallas_call | solution.py:142
  10.9 8.8 %expert_pass.1 = (f32[8,512,1024]{2,1,0:T(8,128)}, bf16[8,128,512]{2,1,0:T(8,128)(2,1)S(1)}, bf16[8,128,512]{2,1,0:T(8,128)(2,1)S(1)}, f32[64,1024]{1,0:T(8,128)...) custom-call(bf16[4,256,64]{2,1,0:T(8,128)(2,1)S(1)} %get-tuple-element.25.pick_ref, ...), custom_call_target="tpu_custom_call" | custom-call | flops 5368709120 | bytes 52428800 | tf_op jit(solution)/shard_map/expert_pass/pallas_call | solution.py:242
  19.7 0.2 collective-permute-start
  19.9 1.7 %collective-permute-start.1 = (f32[64,1024]{1,0:T(8,128)S(1)}, f32[64,1024]{1,0:T(8,128)S(1)}, u32[]{:S(2)}, u32[]{:S(2)}) collective-permute-start(f32[64,1024]{1,0:T(8,128)S(1)} %get-tuple-element.35), channel_id=1, source_target_pairs={{0,2},{1,3},{2,0},{3,1},{4,6},{5,7},{6,4},{7,5},{8,10},{9,11},{10,... | collective-permute-start | bytes 786440 | tf_op jit(solution)/shard_map/ppermute | solution.py:351
  21.6 0.1 collective-permute-start.2
  21.6 11.3 %weight_pass.1 = (f32[8,1024,512]{2,1,0:T(8,128)}, f32[8,1024,512]{2,1,0:T(8,128)}, f32[8,64]{1,0:T(8,128)}) custom-call(bf16[8,128,1024]{2,1,0:T(8,128)(2,1)S(1)} %get-tuple-element.37.x_ref, bf16[8,128,512]{2,1,0:T(8,128)(2,1)S(1)} %get-tuple-element.38.dh1_ref, bf16[8,128,512]{2,1,0:T(8,128)(2,1)S(1)} %get-tuple-element.39.dh3_ref, ...), custom_call_target="tpu_custom_call" | custom-call | flops 2147483648 | bytes 41943040 | tf_op jit(solution)/shard_map/weight_pass/pallas_call | solution.py:321
  32.9 0.0 collective-permute-done
  32.9 0.0 collective-permute-done.1
  32.9 0.6 %collective-permute-done.2 = f32[64,1024]{1,0:T(8,128)S(1)} collective-permute-done((f32[64,1024]{1,0:T(8,128)S(1)}, f32[64,1024]{1,0:T(8,128)S(1)}, u32[]{:S(2)}, u32[]{:S(2)}) %collective-permute-start.2) | collective-permute-done | bytes 262176 | tf_op jit(solution)/shard_map/ppermute | solution.py:351
  33.5 0.7 %add_convert_fusion = bf16[64,1024]{1,0:T(8,128)(2,1)} fusion(f32[64,1024]{1,0:T(8,128)S(1)} %collective-permute-done.2, f32[64,1024]{1,0:T(8,128)S(1)} %collective-permute-done.1, f32[64,1024]{1,0:T(8,128)S(1)} %get-tuple-element.33, f32[64,1024]{1,0:T(8,128)S(1)} %collective-permute-done), kind=kLoop, calls=%fused_computation | loop fusion | flops 262144 | bytes 1179648 | tf_op jit(solution)/shard_map/convert_element_type | solution.py:356
Async XLA Ops:
  19.7 13.2 %collective-permute-start = (f32[64,1024]{1,0:T(8,128)S(1)}, f32[64,1024]{1,0:T(8,128)S(1)}, u32[]{:S(2)}, u32[]{:S(2)}) collective-permute-start(f32[64,1024]{1,0:T(8,128)S(1)} %get-tuple-element.34), channel_id=1, source_target_pairs={{0,1},{1,0},{2,3},{3,2},{4,5},{5,4},{6,7},{7,6},{8,9},{9,8},{10,11... | collective-permute-start | bytes 786440 | tf_op jit(solution)/shard_map/ppermute | solution.py:351
  19.9 13.0 %collective-permute-start.1 = (f32[64,1024]{1,0:T(8,128)S(1)}, f32[64,1024]{1,0:T(8,128)S(1)}, u32[]{:S(2)}, u32[]{:S(2)}) collective-permute-start(f32[64,1024]{1,0:T(8,128)S(1)} %get-tuple-element.35), channel_id=1, source_target_pairs={{0,2},{1,3},{2,0},{3,1},{4,6},{5,7},{6,4},{7,5},{8,10},{9,11},{10,... | collective-permute-start | bytes 786440 | tf_op jit(solution)/shard_map/ppermute | solution.py:351
  21.6 12.0 %collective-permute-start.2 = (f32[64,1024]{1,0:T(8,128)S(1)}, f32[64,1024]{1,0:T(8,128)S(1)}, u32[]{:S(2)}, u32[]{:S(2)}) collective-permute-start(f32[64,1024]{1,0:T(8,128)S(1)} %get-tuple-element.36), channel_id=1, source_target_pairs={{0,3},{1,2},{2,1},{3,0},{4,7},{5,6},{6,5},{7,4},{8,11},{9,10},{10,... | collective-permute-start | bytes 786440 | tf_op jit(solution)/shard_map/ppermute | solution.py:351

commit v6 on v5

--- a/solution.py
+++ b/solution.py
@@ -15,22 +15,24 @@
 MIB = 2**20
 SPLIT = 6
 AHEAD = 3
+LEAD = 2
 
 
 def dot(a, b, ca, cb):
     return lax.dot_general(a, b, (((ca,), (cb,)), ((), ())), preferred_element_type=F32)
 
 
-def front_kernel(n_dev, cap, gy_in, tk_in, sl_in, gt_in, ct_in, hg_in, hu_in, wd_in, wg_in, wu_in, x_in,
-                 gy_ref, pick_ref, d_ref, act_ref, fac1_ref, fac3_ref, wd_ref, wg_ref, wu_ref, x_ref,
+def front_kernel(n_dev, cap, gy_in, tk_in, sl_in, gt_in, ct_in, hg_in, hu_in, wd_in, wg_in, wu_in,
+                 gy_ref, pick_ref, d_ref, act_ref, fac1_ref, fac3_ref, wd_ref, wg_ref, wu_ref,
                  tk_ref, sl_ref, gt_ref, ct_ref, hg_ref, hu_ref, gate_ref, local_sem, load_sem, send_sem, recv_sem):
     me = lax.axis_index("ep")
     n_loc = d_ref.shape[0]
     bufs = [gy_ref, tk_ref, sl_ref, gt_ref, ct_ref]
+    ins = [gy_in, tk_in, sl_in, gt_in, ct_in]
     local = [pltpu.make_async_copy(a, b.at[0], local_sem.at[i])
              for i, (a, b) in enumerate(zip((gy_in, tk_in, sl_in, gt_in, ct_in), bufs))]
     pairs = [(hg_in, hg_ref), (hu_in, hu_ref), (wd_in, wd_ref), (wg_in.at[pl.ds(0, SPLIT)], wg_ref),
-             (wu_in.at[pl.ds(0, SPLIT)], wu_ref), (x_in, x_ref)]
+             (wu_in.at[pl.ds(0, SPLIT)], wu_ref)]
     loads = [pltpu.make_async_copy(a, b, load_sem.at[i]) for i, (a, b) in enumerate(pairs)]
     for cp in local:
         cp.start()
@@ -40,12 +42,10 @@
     for cp in loads:
         cp.start()
     pl.semaphore_wait(barrier, n_dev - 1)
-    for cp in local:
-        cp.wait()
 
     def remote(i, k, src_slot, dst_slot):
         return pltpu.make_async_remote_copy(
-            src_ref=bufs[i].at[src_slot], dst_ref=bufs[i].at[dst_slot],
+            src_ref=bufs[i].at[src_slot] if src_slot else ins[i], dst_ref=bufs[i].at[dst_slot],
             send_sem=send_sem.at[i, dst_slot], recv_sem=recv_sem.at[i, dst_slot],
             device_id={"ep": me ^ k}, device_id_type=MESH)
 
@@ -61,6 +61,8 @@
             cp.start()
     near.start()
 
+    for cp in local:
+        cp.wait()
     loads[0].wait()
     loads[1].wait()
 
@@ -122,8 +124,8 @@
         cp.wait()
 
 
-def front_pass(gy, tk, sl, gt, ct, hg, hu, wd, wg, wu, x, n_dev, cap):
-    args = (gy, tk, sl, gt, ct, hg, hu, wd, wg, wu, x)
+def front_pass(gy, tk, sl, gt, ct, hg, hu, wd, wg, wu, n_dev, cap):
+    args = (gy, tk, sl, gt, ct, hg, hu, wd, wg, wu)
     n_loc, ffn, model = wd.shape
     tok = gy.shape[0]
     rows = hg.shape[1]
@@ -137,7 +139,6 @@
         pltpu.VMEM(wd.shape, BF16),
         pltpu.VMEM((SPLIT,) + wg.shape[1:], BF16),
         pltpu.VMEM((SPLIT,) + wu.shape[1:], BF16),
-        pltpu.VMEM(x.shape, BF16),
     ]
     return pl.pallas_call(
         functools.partial(front_kernel, n_dev, cap),
@@ -153,11 +154,11 @@
             pltpu.VMEM(hu.shape, BF16),
             pltpu.VMEM((n_dev, n_loc * cap, 1), F32),
             pltpu.SemaphoreType.DMA((5,)),
-            pltpu.SemaphoreType.DMA((6,)),
+            pltpu.SemaphoreType.DMA((5,)),
             pltpu.SemaphoreType.DMA((5, n_dev)),
             pltpu.SemaphoreType.DMA((5, n_dev)),
         ],
-        compiler_params=pltpu.CompilerParams(collective_id=0, has_side_effects=True, vmem_limit_bytes=5 * MIB),
+        compiler_params=pltpu.CompilerParams(collective_id=0, has_side_effects=True, vmem_limit_bytes=4 * MIB),
         name="front_pass",
     )(*[pltpu.with_memory_space_constraint(a, pltpu.HBM) for a in args])
 
@@ -182,18 +183,12 @@
         wdt_ref[e % 2] = wd_ref[e].T
 
     def turn_gate_up(e):
-        if e in loads:
-            for cp in loads[e]:
-                cp.wait()
         wg, wu = weights(e)
         wgt_ref[e % 2] = wg.T
         wut_ref[e % 2] = wu[:n_turn].T
 
     def down_grad(e):
-        if e >= n_stage:
-            outs[e - n_stage].wait()
         stage_ref[e % n_stage] = dot(act_ref[e], d_ref[e], 1, 0)
-        outs[e].start()
 
     def hidden_grad(e):
         grad_h = dot(d_ref[e], wd_ref[e], 1, 1) if e == 0 else dot(d_ref[e], wdt_ref[e % 2], 1, 0)
@@ -212,20 +207,34 @@
         for s in range(n_dev):
             ret_ref[s, e * cap:(e + 1) * cap, :] = ret[s * cap:(s + 1) * cap, :]
 
-    down_grad(0)
+    for e in range(LEAD):
+        down_grad(e)
     hidden_grad(0)
     turn_down(1)
-    for e in range(n_loc):
-        if e + AHEAD in loads:
-            for cp in loads[e + AHEAD]:
-                cp.start()
-        if e + 1 < n_loc:
-            down_grad(e + 1)
-            hidden_grad(e + 1)
-            turn_gate_up(e + 1)
-        if e + 2 < n_loc:
-            turn_down(e + 2)
-        row_grad(e)
+    for e in range(0, n_loc, 2):
+        for b in (e, e + 1):
+            if b < n_loc and b < LEAD + e:
+                outs[b].start()
+        for b in (e + AHEAD, e + AHEAD + 1):
+            if b in loads:
+                for cp in loads[b]:
+                    cp.start()
+        for b in (e + LEAD, e + LEAD + 1):
+            if b < n_loc and b >= n_stage:
+                outs[b - n_stage].wait()
+        for b in (e + 1, e + 2):
+            if b in loads:
+                for cp in loads[b]:
+                    cp.wait()
+        for f in (e, e + 1):
+            if f + LEAD < n_loc:
+                down_grad(f + LEAD)
+            if f + 1 < n_loc:
+                hidden_grad(f + 1)
+                turn_gate_up(f + 1)
+            if f + 2 < n_loc:
+                turn_down(f + 2)
+            row_grad(f)
     for k in range(n_dev):
         part_refs[k][...] = dot(pick_ref[k], ret_ref[me ^ k], 0, 0)
     for e in range(n_loc - n_stage, n_loc):
@@ -331,7 +340,7 @@
             pltpu.SemaphoreType.DMA((2, 4)),
             pltpu.SemaphoreType.DMA((2,)),
         ],
-        compiler_params=pltpu.CompilerParams(vmem_limit_bytes=20 * MIB),
+        compiler_params=pltpu.CompilerParams(vmem_limit_bytes=11 * MIB),
         cost_estimate=pl.CostEstimate(flops=4 * n_loc * rows * ffn * model, bytes_accessed=40 * MIB, transcendentals=0),
         name="weight_pass",
     )(x, dh1, dh3, gy, pltpu.with_memory_space_constraint(y, pltpu.HBM))
@@ -345,10 +354,11 @@
 
     def local_step(grad_y, gate_vals, topk_idx, slot_ids, pair_counts, y_routed, x_disp, h_gate, h_up, w_gate, w_up, w_down):
         cap = x_disp.shape[1] // n_dev
-        gy, pick, d, act, fac1, fac3, wd, wga, wua, x = front_pass(
-            grad_y, topk_idx.T, slot_ids.T, gate_vals.T, pair_counts, h_gate, h_up, w_down, w_gate, w_up, x_disp, n_dev, cap)
+        gy, pick, d, act, fac1, fac3, wd, wga, wua = front_pass(
+            grad_y, topk_idx.T, slot_ids.T, gate_vals.T, pair_counts, h_gate, h_up, w_down, w_gate, w_up, n_dev, cap)
         dwd, dh1, dh3, *parts = expert_pass(pick, d, act, fac1, fac3, wd, wga, wua, w_gate, w_up, n_dev, cap)
-        back = [lax.ppermute(parts[k], "ep", [(i, i ^ k) for i in range(n_dev)]) for k in range(1, n_dev)]
+        back = [lax.ppermute(parts[k], "ep", [(i, i ^ k) for i in range(n_dev)]) for k in (2, 3, 1)]
+        x, _ = lax.optimization_barrier((x_disp, parts[0]))
         dwg, dwu, gg = weight_pass(x, dh1, dh3, gy, y_routed)
         total = parts[0]
         for b in back:

time: 34.3 us -> 33.2 us (0.968)
  Pallas kernels: 30.3 us -> 29.4 us
  waiting for transfers between devices: 0.6 us -> 0.09 us
    pallas_call x1, Pallas kernels: 8.83 us -> 8.13 us  [expert_pass(): pl.pallas_call(functools.partial(expert_kernel, n_dev, cap), out_shape=[j...]
    ppermute x3, waiting for transfers between devices: 0.6 us -> 0.09 us  [local_step(): lax.ppermute(parts[k], 'ep', [(i, i ^ k) for i in range(n_dev)])]
  transfers between devices with their start and end apart: 3 -> 3, of which waited for: 1 -> 1; matrix products, arithmetic and copies ran while one was open for 0% -> 0% of each run, Pallas kernels for 33% -> 34%
where the time goes in v6:
time: 33.2 us; the launch traced here: 33.1 us
  Pallas kernels  29.4 us (89%)
  starting transfers between devices  2.18 us (7%)
  other arithmetic  0.72 us (2%)
  between operations  0.68 us (2%)
    pallas_call x1, Pallas kernels, weight_pass(): pl.pallas_call(weight_kernel, out_shape=[grad_shape, grad_shape, jax.Shap...  11.3 us
    pallas_call x1, Pallas kernels, front_pass(): pl.pallas_call(functools.partial(front_kernel, n_dev, cap), out_shape=out...  10 us
    pallas_call x1, Pallas kernels, expert_pass(): pl.pallas_call(functools.partial(expert_kernel, n_dev, cap), out_shape=[j...  8.13 us
    ppermute x3, starting transfers between devices, local_step(): lax.ppermute(parts[k], 'ep', [(i, i ^ k) for i in range(n_dev)])  2.18 us
    convert_element_type x1, other arithmetic, local_step(): return (total.astype(BF16), gg.T, dwg, dwu, dwd)  0.72 us
  transfers between devices with their start and end apart: 3, of which 1 were waited for; matrix products, arithmetic and copies ran while one was open for 0% of the time, Pallas kernels for 34%

profile of v6, /device:TPU:0, one launch (start us, length us, event | category | flops | bytes accessed | tf_op | source)
XLA Modules:
  0.0 33.1 jit_solution(14310177068107457272)
XLA Ops:
  0.6 10.0 %front_pass.1 = (bf16[4,64,1024]{2,1,0:T(8,128)(2,1)S(1)}, bf16[4,256,64]{2,1,0:T(8,128)(2,1)S(1)}, bf16[8,128,1024]{2,1,0:T(8,128)(2,1)S(1)}, bf16[8,512,128]{2...) custom-call(bf16[64,1024]{1,0:T(8,128)(2,1)} %gy_in.1, ...), custom_call_target="tpu_custom_call" | custom-call | tf_op jit(solution)/shard_map/front_pass/pallas_call | solution.py:143
  10.7 0.0 copy-start
  10.7 8.1 %expert_pass.1 = (f32[8,512,1024]{2,1,0:T(8,128)}, bf16[8,128,512]{2,1,0:T(8,128)(2,1)S(1)}, bf16[8,128,512]{2,1,0:T(8,128)(2,1)S(1)}, f32[64,1024]{1,0:T(8,128)...) custom-call(bf16[4,256,64]{2,1,0:T(8,128)(2,1)S(1)} %get-tuple-element.25.pick_ref, ...), custom_call_target="tpu_custom_call" | custom-call | flops 5368709120 | bytes 52428800 | tf_op jit(solution)/shard_map/expert_pass/pallas_call | solution.py:251
  18.8 1.7 %collective-permute-start = (f32[64,1024]{1,0:T(8,128)S(1)}, f32[64,1024]{1,0:T(8,128)S(1)}, u32[]{:S(2)}, u32[]{:S(2)}) collective-permute-start(f32[64,1024]{1,0:T(8,128)S(1)} %get-tuple-element.34), channel_id=1, source_target_pairs={{0,2},{1,3},{2,0},{3,1},{4,6},{5,7},{6,4},{7,5},{8,10},{9,11},{10,... | collective-permute-start | bytes 786440 | tf_op jit(solution)/shard_map/ppermute | solution.py:360
  20.5 0.0 collective-permute-start.1
  20.5 0.5 %collective-permute-start.2 = (f32[64,1024]{1,0:T(8,128)S(1)}, f32[64,1024]{1,0:T(8,128)S(1)}, u32[]{:S(2)}, u32[]{:S(2)}) collective-permute-start(f32[64,1024]{1,0:T(8,128)S(1)} %get-tuple-element.36), channel_id=1, source_target_pairs={{0,1},{1,0},{2,3},{3,2},{4,5},{5,4},{6,7},{7,6},{8,9},{9,8},{10,11... | collective-permute-start | bytes 786440 | tf_op jit(solution)/shard_map/ppermute | solution.py:360
  21.0 0.0 copy-done
  21.0 11.3 %weight_pass.1 = (f32[8,1024,512]{2,1,0:T(8,128)}, f32[8,1024,512]{2,1,0:T(8,128)}, f32[8,64]{1,0:T(8,128)}) custom-call(bf16[8,128,1024]{2,1,0:T(8,128)(2,1)S(1)} %copy-done, bf16[8,128,512]{2,1,0:T(8,128)(2,1)S(1)} %get-tuple-element.38.dh1_ref, bf16[8,128,512]{2,1,0:T(8,128)(2,1)S(1)} %get-tuple-element.39.dh3_ref, ...), custom_call_target="tpu_custom_call" | custom-call | flops 2147483648 | bytes 41943040 | tf_op jit(solution)/shard_map/weight_pass/pallas_call | solution.py:330
  32.3 0.0 collective-permute-done
  32.3 0.1 collective-permute-done.1
  32.4 0.0 collective-permute-done.2
  32.4 0.7 %add_convert_fusion = bf16[64,1024]{1,0:T(8,128)(2,1)} fusion(f32[64,1024]{1,0:T(8,128)S(1)} %collective-permute-done.2, f32[64,1024]{1,0:T(8,128)S(1)} %collective-permute-done.1, f32[64,1024]{1,0:T(8,128)S(1)} %get-tuple-element.33, f32[64,1024]{1,0:T(8,128)S(1)} %collective-permute-done), kind=kLoop, calls=%fused_computation | loop fusion | flops 262144 | bytes 1179648 | tf_op jit(solution)/shard_map/convert_element_type | solution.py:366
Async XLA Ops:
  10.7 10.3 %copy-start = (bf16[8,128,1024]{2,1,0:T(8,128)(2,1)S(1)}, bf16[8,128,1024]{2,1,0:T(8,128)(2,1)}, u32[]{:S(2)}) copy-start(bf16[8,128,1024]{2,1,0:T(8,128)(2,1)} %x_ref) | copy-start | bytes 6291460
  18.8 13.5 %collective-permute-start = (f32[64,1024]{1,0:T(8,128)S(1)}, f32[64,1024]{1,0:T(8,128)S(1)}, u32[]{:S(2)}, u32[]{:S(2)}) collective-permute-start(f32[64,1024]{1,0:T(8,128)S(1)} %get-tuple-element.34), channel_id=1, source_target_pairs={{0,2},{1,3},{2,0},{3,1},{4,6},{5,7},{6,4},{7,5},{8,10},{9,11},{10,... | collective-permute-start | bytes 786440 | tf_op jit(solution)/shard_map/ppermute | solution.py:360
  20.5 11.9 %collective-permute-start.1 = (f32[64,1024]{1,0:T(8,128)S(1)}, f32[64,1024]{1,0:T(8,128)S(1)}, u32[]{:S(2)}, u32[]{:S(2)}) collective-permute-start(f32[64,1024]{1,0:T(8,128)S(1)} %get-tuple-element.35), channel_id=1, source_target_pairs={{0,3},{1,2},{2,1},{3,0},{4,7},{5,6},{6,5},{7,4},{8,11},{9,10},{10,... | collective-permute-start | bytes 786440 | tf_op jit(solution)/shard_map/ppermute | solution.py:360
  20.5 11.8 %collective-permute-start.2 = (f32[64,1024]{1,0:T(8,128)S(1)}, f32[64,1024]{1,0:T(8,128)S(1)}, u32[]{:S(2)}, u32[]{:S(2)}) collective-permute-start(f32[64,1024]{1,0:T(8,128)S(1)} %get-tuple-element.36), channel_id=1, source_target_pairs={{0,1},{1,0},{2,3},{3,2},{4,5},{5,4},{6,7},{7,6},{8,9},{9,8},{10,11... | collective-permute-start | bytes 786440 | tf_op jit(solution)/shard_map/ppermute | solution.py:360

commit v7 on v6

--- a/solution.py
+++ b/solution.py
@@ -15,6 +15,7 @@
 MIB = 2**20
 SPLIT = 6
 AHEAD = 3
+DIRECT = 16
 LEAD = 2
 
 
@@ -24,7 +25,7 @@
 
 def front_kernel(n_dev, cap, gy_in, tk_in, sl_in, gt_in, ct_in, hg_in, hu_in, wd_in, wg_in, wu_in,
                  gy_ref, pick_ref, d_ref, act_ref, fac1_ref, fac3_ref, wd_ref, wg_ref, wu_ref,
-                 tk_ref, sl_ref, gt_ref, ct_ref, hg_ref, hu_ref, gate_ref, local_sem, load_sem, send_sem, recv_sem):
+                 tk_ref, sl_ref, gt_ref, ct_ref, hg_ref, hu_ref, gate_ref, local_sem, load_sem, send_sem, recv_sem, piece_send, piece_recv):
     me = lax.axis_index("ep")
     n_loc = d_ref.shape[0]
     bufs = [gy_ref, tk_ref, sl_ref, gt_ref, ct_ref]
@@ -43,22 +44,32 @@
         cp.start()
     pl.semaphore_wait(barrier, n_dev - 1)
 
-    def remote(i, k, src_slot, dst_slot):
+    def remote(i, k):
         return pltpu.make_async_remote_copy(
-            src_ref=bufs[i].at[src_slot] if src_slot else ins[i], dst_ref=bufs[i].at[dst_slot],
-            send_sem=send_sem.at[i, dst_slot], recv_sem=recv_sem.at[i, dst_slot],
+            src_ref=ins[i], dst_ref=bufs[i].at[k], send_sem=send_sem.at[i, k], recv_sem=recv_sem.at[i, k],
             device_id={"ep": me ^ k}, device_id_type=MESH)
 
-    far = remote(0, 2, 0, 2)
-    near = remote(0, 1, 0, 1)
-    relay = remote(0, 1, 2, 3)
-    small = {k: [remote(i, k, 0, k) for i in range(1, len(bufs))] for k in range(1, n_dev)}
-    for cp in small[2]:
-        cp.start()
-    far.start()
-    for k in (3, 1):
+    def piece(n, k, src, slot, at, size):
+        return pltpu.make_async_remote_copy(
+            src_ref=src.at[pl.ds(at, size)], dst_ref=gy_ref.at[slot, pl.ds(at, size)],
+            send_sem=piece_send.at[n], recv_sem=piece_recv.at[n], device_id={"ep": me ^ k}, device_id_type=MESH)
+
+    tok = gy_in.shape[0]
+    head = tok - DIRECT
+    far_head = piece(0, 2, gy_in, 2, 0, head)
+    far_tail = piece(1, 2, gy_in, 2, head, DIRECT)
+    cross_tail = piece(2, 3, gy_in, 3, head, DIRECT)
+    relay_head = piece(3, 1, gy_ref.at[2], 3, 0, head)
+    near = remote(0, 1)
+    small = {k: [remote(i, k) for i in range(1, len(bufs))] for k in range(1, n_dev)}
+    for k in (2, 3):
         for cp in small[k]:
             cp.start()
+    far_head.start()
+    far_tail.start()
+    cross_tail.start()
+    for cp in small[1]:
+        cp.start()
     near.start()
 
     for cp in local:
@@ -78,7 +89,6 @@
 
     lax.fori_loop(0, n_loc, silu, 0)
 
-    tok = tk_ref.shape[2]
     rows = n_loc * cap
 
     def select(k):
@@ -114,12 +124,15 @@
         select(k)
     near.wait()
     gated_rows(1)
-    far.wait_recv()
-    relay.start()
+    far_head.wait_recv()
+    relay_head.start()
+    far_tail.wait_recv()
     gated_rows(2)
-    relay.wait()
+    cross_tail.wait_recv()
+    relay_head.wait_recv()
     gated_rows(3)
-    far.wait_send()
+    for cp in (far_head, far_tail, cross_tail, relay_head):
+        cp.wait_send()
     for cp in loads[2:]:
         cp.wait()
 
@@ -157,6 +170,8 @@
             pltpu.SemaphoreType.DMA((5,)),
             pltpu.SemaphoreType.DMA((5, n_dev)),
             pltpu.SemaphoreType.DMA((5, n_dev)),
+            pltpu.SemaphoreType.DMA((4,)),
+            pltpu.SemaphoreType.DMA((4,)),
         ],
         compiler_params=pltpu.CompilerParams(collective_id=0, has_side_effects=True, vmem_limit_bytes=4 * MIB),
         name="front_pass",
@@ -229,11 +244,12 @@
         for f in (e, e + 1):
             if f + LEAD < n_loc:
                 down_grad(f + LEAD)
+            if f + 2 < n_loc:
+                turn_down(f + 2)
             if f + 1 < n_loc:
                 hidden_grad(f + 1)
+            if f + 1 < n_loc:
                 turn_gate_up(f + 1)
-            if f + 2 < n_loc:
-                turn_down(f + 2)
             row_grad(f)
     for k in range(n_dev):
         part_refs[k][...] = dot(pick_ref[k], ret_ref[me ^ k], 0, 0)
@@ -264,11 +280,11 @@
             pltpu.VMEM((n_stage, ffn, model), F32),
             pltpu.VMEM((2, model, ffn), BF16),
             pltpu.VMEM((2, ffn, model), BF16),
-            pltpu.VMEM((2, ffn, model // 2), BF16),
+            pltpu.VMEM((2, ffn, model * 5 // 8), BF16),
             pltpu.SemaphoreType.DMA((2, late)),
             pltpu.SemaphoreType.DMA((n_stage,)),
         ],
-        compiler_params=pltpu.CompilerParams(vmem_limit_bytes=(16 + 2 * late) * MIB),
+        compiler_params=pltpu.CompilerParams(vmem_limit_bytes=(16 + 2 * late) * MIB + MIB // 4),
         cost_estimate=pl.CostEstimate(flops=10 * n_loc * rows * ffn * model, bytes_accessed=50 * MIB, transcendentals=0),
         name="expert_pass",
     )(pick, d, act, fac1, fac3, wd, wga, wua, *hbm)

time: 33.2 us -> 32.7 us (0.985)
  Pallas kernels: 29.4 us -> 28.6 us
    pallas_call x1, Pallas kernels: 10 us -> 9.31 us  [front_pass(): pl.pallas_call(functools.partial(front_kernel, n_dev, cap), out_shape=out...]
  transfers between devices with their start and end apart: 3 -> 3, of which waited for: 1 -> 1; matrix products, arithmetic and copies ran while one was open for 0% -> 0% of each run, Pallas kernels for 34% -> 35%
where the time goes in v7:
time: 32.7 us; the launch traced here: 32.6 us
  Pallas kernels  28.6 us (87%)
  starting transfers between devices  2.38 us (7%)
  other arithmetic  0.72 us (2%)
  between operations  0.68 us (2%)
    pallas_call x1, Pallas kernels, weight_pass(): pl.pallas_call(weight_kernel, out_shape=[grad_shape, grad_shape, jax.Shap...  11.3 us
    pallas_call x1, Pallas kernels, front_pass(): pl.pallas_call(functools.partial(front_kernel, n_dev, cap), out_shape=out...  9.31 us
    pallas_call x1, Pallas kernels, expert_pass(): pl.pallas_call(functools.partial(expert_kernel, n_dev, cap), out_shape=[j...  8.06 us
    ppermute x3, starting transfers between devices, local_step(): lax.ppermute(parts[k], 'ep', [(i, i ^ k) for i in range(n_dev)])  2.38 us
    convert_element_type x1, other arithmetic, local_step(): return (total.astype(BF16), gg.T, dwg, dwu, dwd)  0.72 us
  transfers between devices with their start and end apart: 3, of which 1 were waited for; matrix products, arithmetic and copies ran while one was open for 0% of the time, Pallas kernels for 35%

profile of v7, /device:TPU:0, one launch (start us, length us, event | category | flops | bytes accessed | tf_op | source)
XLA Modules:
  0.0 32.6 jit_solution(10640924160467619314)
XLA Ops:
  0.6 9.3 %front_pass.1 = (bf16[4,64,1024]{2,1,0:T(8,128)(2,1)S(1)}, bf16[4,256,64]{2,1,0:T(8,128)(2,1)S(1)}, bf16[8,128,1024]{2,1,0:T(8,128)(2,1)S(1)}, bf16[8,512,128]{2...) custom-call(bf16[64,1024]{1,0:T(8,128)(2,1)} %gy_in.1, ...), custom_call_target="tpu_custom_call" | custom-call | tf_op jit(solution)/shard_map/front_pass/pallas_call | solution.py:156
  10.0 0.0 copy-start
  10.0 8.1 %expert_pass.1 = (f32[8,512,1024]{2,1,0:T(8,128)}, bf16[8,128,512]{2,1,0:T(8,128)(2,1)S(1)}, bf16[8,128,512]{2,1,0:T(8,128)(2,1)S(1)}, f32[64,1024]{1,0:T(8,128)...) custom-call(bf16[4,256,64]{2,1,0:T(8,128)(2,1)S(1)} %get-tuple-element.25.pick_ref, ...), custom_call_target="tpu_custom_call" | custom-call | flops 5368709120 | bytes 52428800 | tf_op jit(solution)/shard_map/expert_pass/pallas_call | solution.py:267
  18.0 2.2 %collective-permute-start = (f32[64,1024]{1,0:T(8,128)S(1)}, f32[64,1024]{1,0:T(8,128)S(1)}, u32[]{:S(2)}, u32[]{:S(2)}) collective-permute-start(f32[64,1024]{1,0:T(8,128)S(1)} %get-tuple-element.34), channel_id=1, source_target_pairs={{0,2},{1,3},{2,0},{3,1},{4,6},{5,7},{6,4},{7,5},{8,10},{9,11},{10,... | collective-permute-start | bytes 786440 | tf_op jit(solution)/shard_map/ppermute | solution.py:376
  20.2 0.0 collective-permute-start.1
  20.2 0.2 collective-permute-start.2
  20.4 0.0 copy-done
  20.4 11.3 %weight_pass.1 = (f32[8,1024,512]{2,1,0:T(8,128)}, f32[8,1024,512]{2,1,0:T(8,128)}, f32[8,64]{1,0:T(8,128)}) custom-call(bf16[8,128,1024]{2,1,0:T(8,128)(2,1)S(1)} %copy-done, bf16[8,128,512]{2,1,0:T(8,128)(2,1)S(1)} %get-tuple-element.38.dh1_ref, bf16[8,128,512]{2,1,0:T(8,128)(2,1)S(1)} %get-tuple-element.39.dh3_ref, ...), custom_call_target="tpu_custom_call" | custom-call | flops 2147483648 | bytes 41943040 | tf_op jit(solution)/shard_map/weight_pass/pallas_call | solution.py:346
  31.7 0.0 collective-permute-done
  31.7 0.2 collective-permute-done.1
  31.9 0.0 collective-permute-done.2
  31.9 0.7 %add_convert_fusion = bf16[64,1024]{1,0:T(8,128)(2,1)} fusion(f32[64,1024]{1,0:T(8,128)S(1)} %collective-permute-done.2, f32[64,1024]{1,0:T(8,128)S(1)} %collective-permute-done.1, f32[64,1024]{1,0:T(8,128)S(1)} %get-tuple-element.33, f32[64,1024]{1,0:T(8,128)S(1)} %collective-permute-done), kind=kLoop, calls=%fused_computation | loop fusion | flops 262144 | bytes 1179648 | tf_op jit(solution)/shard_map/convert_element_type | solution.py:382
Async XLA Ops:
  10.0 10.5 %copy-start = (bf16[8,128,1024]{2,1,0:T(8,128)(2,1)S(1)}, bf16[8,128,1024]{2,1,0:T(8,128)(2,1)}, u32[]{:S(2)}) copy-start(bf16[8,128,1024]{2,1,0:T(8,128)(2,1)} %x_ref) | copy-start | bytes 6291460
  18.0 13.7 %collective-permute-start = (f32[64,1024]{1,0:T(8,128)S(1)}, f32[64,1024]{1,0:T(8,128)S(1)}, u32[]{:S(2)}, u32[]{:S(2)}) collective-permute-start(f32[64,1024]{1,0:T(8,128)S(1)} %get-tuple-element.34), channel_id=1, source_target_pairs={{0,2},{1,3},{2,0},{3,1},{4,6},{5,7},{6,4},{7,5},{8,10},{9,11},{10,... | collective-permute-start | bytes 786440 | tf_op jit(solution)/shard_map/ppermute | solution.py:376
  20.2 11.7 %collective-permute-start.1 = (f32[64,1024]{1,0:T(8,128)S(1)}, f32[64,1024]{1,0:T(8,128)S(1)}, u32[]{:S(2)}, u32[]{:S(2)}) collective-permute-start(f32[64,1024]{1,0:T(8,128)S(1)} %get-tuple-element.35), channel_id=1, source_target_pairs={{0,3},{1,2},{2,1},{3,0},{4,7},{5,6},{6,5},{7,4},{8,11},{9,10},{10,... | collective-permute-start | bytes 786440 | tf_op jit(solution)/shard_map/ppermute | solution.py:376
  20.2 11.7 %collective-permute-start.2 = (f32[64,1024]{1,0:T(8,128)S(1)}, f32[64,1024]{1,0:T(8,128)S(1)}, u32[]{:S(2)}, u32[]{:S(2)}) collective-permute-start(f32[64,1024]{1,0:T(8,128)S(1)} %get-tuple-element.36), channel_id=1, source_target_pairs={{0,1},{1,0},{2,3},{3,2},{4,5},{5,4},{6,7},{7,6},{8,9},{9,8},{10,11... | collective-permute-start | bytes 786440 | tf_op jit(solution)/shard_map/ppermute | solution.py:376

commit v8 on v7

--- a/solution.py
+++ b/solution.py
@@ -14,7 +14,7 @@
 VMEM = pl.BlockSpec(memory_space=pltpu.VMEM)
 MIB = 2**20
 SPLIT = 6
-AHEAD = 3
+AHEAD = 4
 DIRECT = 16
 LEAD = 2
 
@@ -242,10 +242,10 @@
                 for cp in loads[b]:
                     cp.wait()
         for f in (e, e + 1):
+            if f + 2 < n_loc:
+                turn_down(f + 2)
             if f + LEAD < n_loc:
                 down_grad(f + LEAD)
-            if f + 2 < n_loc:
-                turn_down(f + 2)
             if f + 1 < n_loc:
                 hidden_grad(f + 1)
             if f + 1 < n_loc:

time: 32.7 us -> 32.7 us (level)
  no operation moved by 1% of the time
where the time goes in v8:
time: 32.7 us; the launch traced here: 32.6 us
  Pallas kernels  28.6 us (87%)
  starting transfers between devices  2.38 us (7%)
  other arithmetic  0.72 us (2%)
  between operations  0.68 us (2%)
    pallas_call x1, Pallas kernels, weight_pass(): pl.pallas_call(weight_kernel, out_shape=[grad_shape, grad_shape, jax.Shap...  11.3 us
    pallas_call x1, Pallas kernels, front_pass(): pl.pallas_call(functools.partial(front_kernel, n_dev, cap), out_shape=out...  9.31 us
    pallas_call x1, Pallas kernels, expert_pass(): pl.pallas_call(functools.partial(expert_kernel, n_dev, cap), out_shape=[j...  8.02 us
    ppermute x3, starting transfers between devices, local_step(): lax.ppermute(parts[k], 'ep', [(i, i ^ k) for i in range(n_dev)])  2.38 us
    convert_element_type x1, other arithmetic, local_step(): return (total.astype(BF16), gg.T, dwg, dwu, dwd)  0.72 us
  transfers between devices with their start and end apart: 3, of which 1 were waited for; matrix products, arithmetic and copies ran while one was open for 0% of the time, Pallas kernels for 35%

profile of v8, /device:TPU:0, one launch (start us, length us, event | category | flops | bytes accessed | tf_op | source)
XLA Modules:
  0.0 32.6 jit_solution(6333254993693872583)
XLA Ops:
  0.6 9.3 %front_pass.1 = (bf16[4,64,1024]{2,1,0:T(8,128)(2,1)S(1)}, bf16[4,256,64]{2,1,0:T(8,128)(2,1)S(1)}, bf16[8,128,1024]{2,1,0:T(8,128)(2,1)S(1)}, bf16[8,512,128]{2...) custom-call(bf16[64,1024]{1,0:T(8,128)(2,1)} %gy_in.1, ...), custom_call_target="tpu_custom_call" | custom-call | tf_op jit(solution)/shard_map/front_pass/pallas_call | solution.py:156
  10.0 0.0 copy-start
  10.0 8.0 %expert_pass.1 = (f32[8,512,1024]{2,1,0:T(8,128)}, bf16[8,128,512]{2,1,0:T(8,128)(2,1)S(1)}, bf16[8,128,512]{2,1,0:T(8,128)(2,1)S(1)}, f32[64,1024]{1,0:T(8,128)...) custom-call(bf16[4,256,64]{2,1,0:T(8,128)(2,1)S(1)} %get-tuple-element.25.pick_ref, ...), custom_call_target="tpu_custom_call" | custom-call | flops 5368709120 | bytes 52428800 | tf_op jit(solution)/shard_map/expert_pass/pallas_call | solution.py:267
  18.0 2.2 %collective-permute-start = (f32[64,1024]{1,0:T(8,128)S(1)}, f32[64,1024]{1,0:T(8,128)S(1)}, u32[]{:S(2)}, u32[]{:S(2)}) collective-permute-start(f32[64,1024]{1,0:T(8,128)S(1)} %get-tuple-element.34), channel_id=1, source_target_pairs={{0,2},{1,3},{2,0},{3,1},{4,6},{5,7},{6,4},{7,5},{8,10},{9,11},{10,... | collective-permute-start | bytes 786440 | tf_op jit(solution)/shard_map/ppermute | solution.py:376
  20.2 0.0 collective-permute-start.1
  20.2 0.2 collective-permute-start.2
  20.4 0.0 copy-done
  20.4 11.3 %weight_pass.1 = (f32[8,1024,512]{2,1,0:T(8,128)}, f32[8,1024,512]{2,1,0:T(8,128)}, f32[8,64]{1,0:T(8,128)}) custom-call(bf16[8,128,1024]{2,1,0:T(8,128)(2,1)S(1)} %copy-done, bf16[8,128,512]{2,1,0:T(8,128)(2,1)S(1)} %get-tuple-element.38.dh1_ref, bf16[8,128,512]{2,1,0:T(8,128)(2,1)S(1)} %get-tuple-element.39.dh3_ref, ...), custom_call_target="tpu_custom_call" | custom-call | flops 2147483648 | bytes 41943040 | tf_op jit(solution)/shard_map/weight_pass/pallas_call | solution.py:346
  31.7 0.0 collective-permute-done
  31.7 0.2 collective-permute-done.1
  31.9 0.0 collective-permute-done.2
  31.9 0.7 %add_convert_fusion = bf16[64,1024]{1,0:T(8,128)(2,1)} fusion(f32[64,1024]{1,0:T(8,128)S(1)} %collective-permute-done.2, f32[64,1024]{1,0:T(8,128)S(1)} %collective-permute-done.1, f32[64,1024]{1,0:T(8,128)S(1)} %get-tuple-element.33, f32[64,1024]{1,0:T(8,128)S(1)} %collective-permute-done), kind=kLoop, calls=%fused_computation | loop fusion | flops 262144 | bytes 1179648 | tf_op jit(solution)/shard_map/convert_element_type | solution.py:382
Async XLA Ops:
  10.0 10.4 %copy-start = (bf16[8,128,1024]{2,1,0:T(8,128)(2,1)S(1)}, bf16[8,128,1024]{2,1,0:T(8,128)(2,1)}, u32[]{:S(2)}) copy-start(bf16[8,128,1024]{2,1,0:T(8,128)(2,1)} %x_ref) | copy-start | bytes 6291460
  18.0 13.7 %collective-permute-start = (f32[64,1024]{1,0:T(8,128)S(1)}, f32[64,1024]{1,0:T(8,128)S(1)}, u32[]{:S(2)}, u32[]{:S(2)}) collective-permute-start(f32[64,1024]{1,0:T(8,128)S(1)} %get-tuple-element.34), channel_id=1, source_target_pairs={{0,2},{1,3},{2,0},{3,1},{4,6},{5,7},{6,4},{7,5},{8,10},{9,11},{10,... | collective-permute-start | bytes 786440 | tf_op jit(solution)/shard_map/ppermute | solution.py:376
  20.2 11.7 %collective-permute-start.1 = (f32[64,1024]{1,0:T(8,128)S(1)}, f32[64,1024]{1,0:T(8,128)S(1)}, u32[]{:S(2)}, u32[]{:S(2)}) collective-permute-start(f32[64,1024]{1,0:T(8,128)S(1)} %get-tuple-element.35), channel_id=1, source_target_pairs={{0,3},{1,2},{2,1},{3,0},{4,7},{5,6},{6,5},{7,4},{8,11},{9,10},{10,... | collective-permute-start | bytes 786440 | tf_op jit(solution)/shard_map/ppermute | solution.py:376
  20.2 11.7 %collective-permute-start.2 = (f32[64,1024]{1,0:T(8,128)S(1)}, f32[64,1024]{1,0:T(8,128)S(1)}, u32[]{:S(2)}, u32[]{:S(2)}) collective-permute-start(f32[64,1024]{1,0:T(8,128)S(1)} %get-tuple-element.36), channel_id=1, source_target_pairs={{0,1},{1,0},{2,3},{3,2},{4,5},{5,4},{6,7},{7,6},{8,9},{9,8},{10,11... | collective-permute-start | bytes 786440 | tf_op jit(solution)/shard_map/ppermute | solution.py:376
